TPU v7x, 32 devices: a whole 2x2x4 slice. The times are simulated.
32 devices in a mesh: dp: 2 (over x), dm: 4 (over z), tp: 4 (over y, core).
Axes of the slice: x: 2, y: 2, z: 4, core: 2. Of those that a mesh axis runs over, the one named last changes fastest.
Arguments:
- hidden: bfloat16 [128, 3072], P('dp', 'dm'), parts along dimension 0
- w_q: bfloat16 [3072, 24, 128], P('dm', 'tp')
- w_k: bfloat16 [3072, 8, 128], P('dm', 'tp')
- w_v: bfloat16 [3072, 8, 128], P('dm', 'tp')
- w_o: bfloat16 [24, 128, 3072], P('tp', None, 'dm')
- w_gate: bfloat16 [3072, 8192], P('dm', 'tp')
- w_up: bfloat16 [3072, 8192], P('dm', 'tp')
- w_down: bfloat16 [8192, 3072], P('tp', 'dm')
- norm_attn: bfloat16 [3072], P('dm')
- norm_mlp: bfloat16 [3072], P('dm')
- k_cache: bfloat16 [128, 1024, 8, 128], P(('dp', 'dm'), None, 'tp'), parts along dimension 0
- v_cache: bfloat16 [128, 1024, 8, 128], P(('dp', 'dm'), None, 'tp'), parts along dimension 0
- seq_lens: int32 [128], P(('dp', 'dm')), parts along dimension 0
- rope_cos: float32 [128, 64], P(('dp', 'dm')), parts along dimension 0
- rope_sin: float32 [128, 64], P(('dp', 'dm')), parts along dimension 0
Outputs:
- output 1: bfloat16 [128, 3072], P('dp', 'dm'), parts along dimension 0
- output 2: bfloat16 [128, 1024, 8, 128], P(('dp', 'dm'), None, 'tp'), parts along dimension 0
- output 3: bfloat16 [128, 1024, 8, 128], P(('dp', 'dm'), None, 'tp'), parts along dimension 0
There are 2 independent parts. A program takes and returns all parts, laid end to end along the dimension named above; an argument that names none is the same for every part.
All inputs are finite; a program needn't handle non-finite values.
Results may differ from a plain program's by a relative error of at most 0.0107316.
Values are sent between devices in bfloat16 or wider.
A program may use at most 1 GiB of HBM per device.

v0:
```python
import jax
import jax.numpy as jnp
from jax import lax
from jax.sharding import PartitionSpec as P

EPS = 1e-6


def width_norm(x, gain, width_full):
    x_f32 = x.astype(jnp.float32)
    sq_sum = lax.psum(jnp.sum(x_f32 * x_f32, axis=-1, keepdims=True), 'dm')
    scale = lax.rsqrt(sq_sum / width_full + EPS)
    return (x_f32 * scale * gain.astype(jnp.float32)).astype(jnp.bfloat16)


def apply_rope(x, rope_cos, rope_sin):
    half = x.shape[-1] // 2
    first = x[..., :half]
    second = x[..., half:]
    cosine = rope_cos[:, None, :]
    sine = rope_sin[:, None, :]
    return jnp.concatenate([first * cosine - second * sine, second * cosine + first * sine], axis=-1).astype(jnp.bfloat16)


def attend(q_rot, k_rot, v_new, k_cache, v_cache, seq_lens):
    rows, seq_len, kv_local, head_dim = k_cache.shape
    positions = jnp.arange(seq_len)
    write_mask = (positions[None, :] == seq_lens[:, None])[:, :, None, None]
    k_out = jnp.where(write_mask, k_rot[:, None], k_cache)
    v_out = jnp.where(write_mask, v_new[:, None], v_cache)
    q_grp = q_rot.reshape(rows, kv_local, -1, head_dim)
    scores = jnp.einsum('bkgd,bskd->bkgs', q_grp, k_out, preferred_element_type=jnp.float32) * (head_dim ** -0.5)
    key_mask = (positions[None, :] <= seq_lens[:, None])[:, None, None, :]
    scores = jnp.where(key_mask, scores, -1e30)
    attn_probs = jax.nn.softmax(scores, axis=-1).astype(jnp.bfloat16)
    heads = jnp.einsum('bkgs,bskd->bkgd', attn_probs, v_out, preferred_element_type=jnp.float32)
    return heads.astype(jnp.bfloat16).reshape(rows, -1, head_dim), k_out, v_out


def solution(mesh):
    width_shards = mesh.shape['dm']
    row_spec = P('dp', 'dm')
    cache_spec = P(('dp', 'dm'), None, 'tp', None)
    batch_spec = P(('dp', 'dm'))
    rope_spec = P(('dp', 'dm'), None)
    in_specs = (row_spec, P('dm', 'tp', None), P('dm', 'tp', None), P('dm', 'tp', None), P('tp', None, 'dm'), P('dm', 'tp'), P('dm', 'tp'), P('tp', 'dm'), P('dm'), P('dm'), cache_spec, cache_spec, batch_spec, rope_spec, rope_spec)
    out_specs = (row_spec, cache_spec, cache_spec)

    def local_layer(hidden, w_q, w_k, w_v, w_o, w_gate, w_up, w_down, norm_attn, norm_mlp, k_cache, v_cache, seq_lens, rope_cos, rope_sin):
        width_full = hidden.shape[1] * width_shards
        x_norm = width_norm(hidden, norm_attn, width_full)
        q_part = jnp.einsum('bd,dhk->bhk', x_norm, w_q, preferred_element_type=jnp.float32)
        k_part = jnp.einsum('bd,dhk->bhk', x_norm, w_k, preferred_element_type=jnp.float32)
        v_part = jnp.einsum('bd,dhk->bhk', x_norm, w_v, preferred_element_type=jnp.float32)
        q_rows = lax.psum_scatter(q_part, 'dm', scatter_dimension=0, tiled=True)
        k_rows = lax.psum_scatter(k_part, 'dm', scatter_dimension=0, tiled=True)
        v_rows = lax.psum_scatter(v_part, 'dm', scatter_dimension=0, tiled=True)
        q_rot = apply_rope(q_rows, rope_cos, rope_sin)
        k_rot = apply_rope(k_rows, rope_cos, rope_sin)
        attn_heads, k_out, v_out = attend(q_rot, k_rot, v_rows.astype(jnp.bfloat16), k_cache, v_cache, seq_lens)
        heads_all = lax.all_gather(attn_heads, 'dm', axis=0, tiled=True)
        attn_part = jnp.einsum('bhk,hkd->bd', heads_all, w_o, preferred_element_type=jnp.float32)
        attn_out = lax.psum(attn_part, 'tp').astype(jnp.bfloat16)
        h_mid = hidden + attn_out
        x_mlp = width_norm(h_mid, norm_mlp, width_full)
        gate = lax.psum(jnp.dot(x_mlp, w_gate, preferred_element_type=jnp.float32), 'dm')
        up_proj = lax.psum(jnp.dot(x_mlp, w_up, preferred_element_type=jnp.float32), 'dm')
        gated_act = (jax.nn.silu(gate) * up_proj).astype(jnp.bfloat16)
        mlp_out = lax.psum(jnp.dot(gated_act, w_down, preferred_element_type=jnp.float32), 'tp').astype(jnp.bfloat16)
        return h_mid + mlp_out, k_out, v_out

    return jax.shard_map(local_layer, mesh=mesh, in_specs=in_specs, out_specs=out_specs, check_vma=False)
```

profile of v0, /device:TPU:0, one launch (start us, length us, event | category | flops | bytes accessed | tf_op | source)
XLA Modules:
  0.0 218.9 jit_solution(8004687340210166689)
XLA Ops:
  7.2 0.0 copy-start
  7.2 0.0 reduce-scatter.6.cloned.1.call-start
  7.2 1.2 fusion.23
  8.4 13.5 %psum.42 = f32[64,1]{0,1:T(1,128)S(1)} all-reduce(f32[64,1]{0,1:T(1,128)S(1)} %bitcast.26), channel_id=1, replica_groups=mesh['dp'=2,'dm'=4,'tp'=4] {'dm'}, use_global_device_ids=true, to_apply=%region_1.0 | all-reduce | flops 64 | bytes 512 | tf_op jit(solution)/shard_map/psum | solution.py:11
  21.9 0.7 convert_element_type.44
  22.6 1.9 fusion.18
  24.5 0.0 reduce-scatter.6.cloned.1.call-update
  24.6 0.0 reduce-scatter.8.cloned.1.call-start
  24.6 1.9 fusion.16
  26.5 0.0 reduce-scatter.8.cloned.1.call-update
  26.6 0.0 reduce-scatter.4.cloned.1.call-start
  26.6 2.4 %fusion.39 = f32[64,6,128]{2,0,1:T(8,128)} fusion(bf16[768,6,128]{2,0,1:T(8,128)(2,1)} %param.16, bf16[64,768]{1,0:T(8,128)(2,1)} %param.15, f32[768]{0:T(1024)S(1)} %convert_element_type.44, f32[64]{0:T(128)S(1)} %rsqrt_bitcast_fusion.1), kind=kOutput, calls=%fused_computation.47 | convolution fusion | flops 75694080 | bytes 1477888 | tf_op jit(solution)/shard_map/bd,dhk->bhk/dot_general | solution.py:52
  29.0 0.0 reduce-scatter.4.cloned.1.call-update
  29.0 0.0 all-reduce.5.cloned.1.call-start
  29.1 0.7 convert_element_type.51
  29.7 0.7 iota_compare_fusion.1
  30.5 11.7 %reduce-scatter.6.cloned.1.call-done = f32[16,2,128]{2,0,1:T(8,128)} async-done(((f32[64,2,128]{2,0,1:T(8,128)}), f32[16,2,128]{2,0,1:T(8,128)}) %reduce-scatter.6.cloned.1.call-update) | async-done | bytes 16400 | tf_op jit(solution)/shard_map/reduce_scatter | solution.py:56
  42.2 0.9 subtract_convert_fusion.1
  43.0 0.1 pad_maximum_fusion
  43.1 19.3 %reduce-scatter.8.cloned.1.call-done = f32[16,2,128]{2,0,1:T(8,128)} async-done(((f32[64,2,128]{2,0,1:T(8,128)}), f32[16,2,128]{2,0,1:T(8,128)}) %reduce-scatter.8.cloned.1.call-update) | async-done | bytes 16400 | tf_op jit(solution)/shard_map/reduce_scatter | solution.py:57
  62.4 0.7 convert_element_type.47
  63.2 0.0 copy-start.3
  63.2 0.0 copy-start.4
  63.2 26.3 %broadcast_select_fusion.1 = (bf16[16,1024,2,128]{3,2,1,0:T(2,128)(2,1)}, bf16[16,1024,2,128]{3,2,1,0:T(2,128)(2,1)}) fusion(bf16[16,1024,2,128]{3,2,1,0:T(2,128)(2,1)} %param.25, pred[16,1024]{1,0:T(8,128)(4,1)S(1)} %get-tuple-element.14, bf16[16,2,128]{2,1,0:T(2,128)(2,1)S(1)} %copy.30, bf16[16,1024,2,128]{3,2,1,0:T(2,128)(2,1)} %param.26, ...), kind=kLoop, calls=%fused_computation.2 | loop fusion | flops 8388608 | bytes 33587200 | tf_op jit(solution)/shard_map/jit(_where)/select_n | solution.py:29
  89.5 0.0 reduce-scatter.4.cloned.1.call-done
  89.5 0.0 copy-done.3
  89.5 0.0 copy-done.4
  89.6 1.0 subtract_convert_fusion
  90.6 6.6 %fusion.43 = (f32[16,2,3]{2,1,0:T(2,128)S(1)}, f32[16,2,3,1024]{3,2,1,0:T(4,128)}) fusion(bf16[16,1024,2,128]{3,2,1,0:T(2,128)(2,1)} %get-tuple-element.11, pred[16,1024]{1,0:T(8,128)(4,1)S(1)} %get-tuple-element.13, bf16[16,2,3,64]{3,2,1,0:T(4,128)(2,1)S(1)} %copy.28, bf16[16,2,3,64]{3,2,1,0:T(4,128)(2,1)S(1)} %copy.27), kind=kOutput, calls=%fused_computation.52 | convolution fusion | flops 25609216 | bytes 8823168 | tf_op jit(solution)/shard_map/sub | solution.py:35
  97.2 0.0 copy-start.1
  97.2 0.0 copy-start.2
  97.2 5.0 %fusion.10 = bf16[16,2,3,128]{3,2,1,0:T(4,128)(2,1)S(1)} fusion(bf16[16,1024,2,128]{3,2,1,0:T(2,128)(2,1)} %get-tuple-element.12, f32[16,2,3,1024]{3,2,1,0:T(4,128)} %get-tuple-element.16, f32[16,2,3]{2,1,0:T(2,128)S(1)} %get-tuple-element.15), kind=kOutput, calls=%fused_computation.11 | convolution fusion | flops 25374720 | bytes 8806784 | tf_op jit(solution)/shard_map/bkgs,bskd->bkgd/dot_general | solution.py:36
  102.2 13.2 %all_gather.3 = bf16[64,6,128]{2,0,1:T(8,128)(2,1)S(1)} all-gather(bf16[16,6,128]{2,0,1:T(8,128)(2,1)S(1)} %bitcast.24), channel_id=1, replica_groups=mesh['dp'=2,'dm'=4,'tp'=4] {'dm'}, dimensions={0}, use_global_device_ids=true | all-gather | bytes 122880 | tf_op jit(solution)/shard_map/all_gather | solution.py:61
  115.5 0.0 copy-done.1
  115.5 0.3 convolution_bitcast_fusion
  115.8 12.6 %all-reduce.6 = bf16[64,768]{1,0:T(8,128)(2,1)} all-reduce(f32[64,768]{1,0:T(8,128)S(1)} %convolution_bitcast_fusion), channel_id=1, replica_groups=mesh['dp'=2,'dm'=4,'tp'=4] {'tp'}, use_global_device_ids=true, to_apply=%region_7.8 | all-reduce | flops 49152 | bytes 294912 | tf_op jit(solution)/shard_map/psum | solution.py:63
  128.4 0.0 copy-done.2
  128.4 1.0 fusion.26
  129.4 8.9 %psum.44 = f32[64,1]{0,1:T(1,128)S(1)} all-reduce(f32[64,1]{0,1:T(1,128)S(1)} %bitcast.25), channel_id=1, replica_groups=mesh['dp'=2,'dm'=4,'tp'=4] {'dm'}, use_global_device_ids=true, to_apply=%region_9.10 | all-reduce | flops 64 | bytes 512 | tf_op jit(solution)/shard_map/psum | solution.py:11
  138.4 0.0 copy-done
  138.4 1.5 fusion.33
  139.9 3.4 %fusion.35 = f32[64,2048]{1,0:T(8,128)} fusion(bf16[768,2048]{1,0:T(8,128)(2,1)} %param.20, bf16[64,768]{1,0:T(8,128)(2,1)S(1)} %get-tuple-element.6, f32[768]{0:T(1024)S(1)} %convert_element_type.51, f32[64]{0:T(128)S(1)} %rsqrt_bitcast_fusion), kind=kOutput, calls=%fused_computation.43 | convolution fusion | flops 201523200 | bytes 3771648 | tf_op jit(solution)/shard_map/dot_general | solution.py:66
  143.3 0.0 all-reduce.5.cloned.1.call-update
  143.3 51.9 %all-reduce.5.cloned.1.call-done = (f32[64,2048]{1,0:T(8,128)}, f32[64,2048]{1,0:T(8,128)}) async-done(((f32[64,2048]{1,0:T(8,128)}, f32[64,2048]{1,0:T(8,128)}), (f32[64,2048]{1,0:T(8,128)}, f32[64,2048]{1,0:T(8,128)})) %all-reduce.5.cloned.1.call-update) | async-done | bytes 1048592 | tf_op jit(solution)/shard_map/psum | solution.py:67
  195.2 2.9 %fusion.20 = f32[64,768]{1,0:T(8,128)S(1)} fusion(bf16[2048,768]{1,0:T(8,128)(2,1)} %param.22, f32[64,2048]{1,0:T(8,128)} %get-tuple-element.3, f32[64,2048]{1,0:T(8,128)} %get-tuple-element.4), kind=kOutput, calls=%fused_computation.19 | convolution fusion | flops 202113024 | bytes 4390912 | tf_op jit(solution)/shard_map/dot_general | solution.py:69
  198.1 13.6 %all-reduce.7 = bf16[64,768]{1,0:T(8,128)(2,1)S(1)} all-reduce(f32[64,768]{1,0:T(8,128)S(1)} %fusion.20), channel_id=1, replica_groups=mesh['dp'=2,'dm'=4,'tp'=4] {'tp'}, use_global_device_ids=true, to_apply=%region_12.13 | all-reduce | flops 49152 | bytes 294912 | tf_op jit(solution)/shard_map/psum | solution.py:69
  211.7 0.7 add.55
  (7 shorter events, 0.1 us)
Async XLA Ops:
  7.2 131.2 %copy-start = (bf16[768,2048]{1,0:T(8,128)(2,1)S(1)}, bf16[768,2048]{1,0:T(8,128)(2,1)}, u32[]{:S(2)}) copy-start(bf16[768,2048]{1,0:T(8,128)(2,1)} %param.21) | copy-start | bytes 9437188
  7.2 35.0 %reduce-scatter.6.cloned.1.call-start = ((), (), s32[]{:S(2)}) async-start(), calls=%async_computation.4 | async-start | bytes 81920 | tf_op jit(solution)/shard_map/reduce_scatter | solution.py:56
  24.6 37.9 %reduce-scatter.8.cloned.1.call-start = ((), (), s32[]{:S(2)}) async-start(), calls=%async_computation.5 | async-start | bytes 81920 | tf_op jit(solution)/shard_map/reduce_scatter | solution.py:57
  26.6 63.0 %reduce-scatter.4.cloned.1.call-start = ((), (), s32[]{:S(2)}) async-start(), calls=%async_computation.3 | async-start | bytes 245760 | tf_op jit(solution)/shard_map/reduce_scatter | solution.py:55
  29.0 166.2 %all-reduce.5.cloned.1.call-start = ((), (), s32[]{:S(2)}) async-start(), calls=%async_computation.6 | async-start | bytes 2097152 | tf_op jit(solution)/shard_map/psum | solution.py:67
  63.2 26.4 %copy-start.3 = (f32[16,64]{1,0:T(8,128)S(1)}, f32[16,64]{1,0:T(8,128)}, u32[]{:S(2)}) copy-start(f32[16,64]{1,0:T(8,128)} %param.29) | copy-start | bytes 12292
  63.2 26.4 %copy-start.4 = (f32[16,64]{1,0:T(8,128)S(1)}, f32[16,64]{1,0:T(8,128)}, u32[]{:S(2)}) copy-start(f32[16,64]{1,0:T(8,128)} %param.28) | copy-start | bytes 12292
  97.2 18.3 %copy-start.1 = (bf16[6,128,768]{2,1,0:T(8,128)(2,1)S(1)}, bf16[6,128,768]{2,1,0:T(8,128)(2,1)}, u32[]{:S(2)}) copy-start(bf16[6,128,768]{2,1,0:T(8,128)(2,1)} %param.19) | copy-start | bytes 3538948
  97.2 31.2 %copy-start.2 = (bf16[64,768]{1,0:T(8,128)(2,1)S(1)}, bf16[64,768]{1,0:T(8,128)(2,1)}, u32[]{:S(2)}) copy-start(bf16[64,768]{1,0:T(8,128)(2,1)} %param.15) | copy-start | bytes 294916
Sparse Core Ops, SparseCore 0:
  24.7 17.4 reduce-scatter.5
  45.0 17.4 reduce-scatter.7
  64.7 17.6 reduce-scatter.3
  143.4 51.7 all-reduce.4
where the time goes:
time: 220 us; the launch traced here: 219 us
  waiting for transfers between devices  83 us (38%)
  blocking collectives  61.9 us (28%)
  other arithmetic  33.9 us (15%)
  matrix products  26 us (12%)
  between operations  13.9 us (6%)
    psum x1, waiting for transfers between devices, local_layer(): lax.psum(jnp.dot(x_mlp, w_up, preferred_element_type=jnp.float32), 'dm')  51.9 us
    select_n x1, other arithmetic, attend(): k_out = jnp.where(write_mask, k_rot[:, None], k_cache)  26.3 us
    psum x2, blocking collectives, width_norm(): sq_sum = lax.psum(jnp.sum(x_f32 * x_f32, axis=-1, keepdims=True), 'dm')  22.4 us
    reduce_scatter x1, waiting for transfers between devices, local_layer(): v_rows = lax.psum_scatter(v_part, 'dm', scatter_dimension=0, tiled=True)  19.3 us
    psum x1, blocking collectives, local_layer(): lax.psum(jnp.dot(gated_act, w_down, preferred_element_type=jnp.float32),...  13.6 us
    all_gather x1, blocking collectives, local_layer(): heads_all = lax.all_gather(attn_heads, 'dm', axis=0, tiled=True)  13.2 us
    psum x1, blocking collectives, local_layer(): attn_out = lax.psum(attn_part, 'tp').astype(jnp.bfloat16)  12.6 us
    reduce_scatter x1, waiting for transfers between devices, local_layer(): k_rows = lax.psum_scatter(k_part, 'dm', scatter_dimension=0, tiled=True)  11.7 us
  transfers between devices with their start and end apart: 4, of which 3 were waited for; matrix products, arithmetic and copies ran while one was open for 15% of the time, Pallas kernels for 0%

commit v1 on v0

v1 whole, which is shorter than its diff:
```python
import jax
import jax.numpy as jnp
from jax import lax
from jax.experimental import pallas as pl
from jax.experimental.pallas import tpu as pltpu
from jax.sharding import PartitionSpec as P

EPS = 1e-6
F32 = jnp.float32
BF16 = jnp.bfloat16
MESH = pl.DeviceIdType.MESH
ANY = pl.BlockSpec(memory_space=pl.ANY)
VM = pl.BlockSpec(memory_space=pltpu.VMEM)
SM = pl.BlockSpec(memory_space=pltpu.SMEM)
DMA = pltpu.SemaphoreType.DMA

NZ = 4
NT = 4
ROWS = 64
RB = 16
W = 768
HD = 128
NH = 6
GRP = 3
SEQ2 = 2048
QKV = (NH + 4) * HD
PAY = QKV + HD
FFL = 2048
NP = 8
PC = 128


def partners(i):
    return (3 - i, (i + 2) % 4, i + 1 - 2 * (i % 2))


def dot(a, b):
    return jnp.dot(a, b, preferred_element_type=F32)


def local_scale(x, width):
    ss = jnp.sum(x * x, axis=-1, keepdims=True)
    return ss, lax.rsqrt(ss / width + EPS)


def qkv_kernel(hid, gain, wq, wk, wv, cos, sin, kc, vc,
               q_o, k_o, v_o, kc_o, vc_o,
               h_s, g_s, wq_s, wk_s, wv_s, cos_s, sin_s, part, recv,
               in_sem, c_sem, send_sem, recv_sem):
    z = lax.axis_index('dm')
    peers = partners(z)
    ins = [pltpu.make_async_copy(s, d, in_sem.at[i]) for i, (s, d) in enumerate(
        ((hid, h_s), (gain, g_s), (wk, wk_s), (wv, wv_s), (wq, wq_s), (cos, cos_s), (sin, sin_s)))]
    for c in ins:
        c.start()
    caches = [pltpu.make_async_copy(kc, kc_o, c_sem.at[0]), pltpu.make_async_copy(vc, vc_o, c_sem.at[1])]
    for c in caches:
        c.start()
    barrier = pltpu.get_barrier_semaphore()
    for p in peers:
        pl.semaphore_signal(barrier, inc=1, device_id={'dm': p}, device_id_type=MESH)

    ins[0].wait()
    ins[1].wait()
    h = h_s[...].astype(F32)
    ss, scale = local_scale(h, W)
    part[:, QKV:PAY] = jnp.broadcast_to(ss, (ROWS, HD))
    x = (h * scale * g_s[...].astype(F32).reshape(1, W)).astype(BF16)
    rr = lax.broadcasted_iota(jnp.int32, (HD, 2 * HD), 0)
    cc = lax.broadcasted_iota(jnp.int32, (HD, 2 * HD), 1)
    spread = []
    for hd in range(2):
        sel = jnp.where(cc == 2 * rr + hd, 1.0, 0.0).astype(BF16)
        spread.append(jnp.concatenate(
            [dot(x[:, j * HD:(j + 1) * HD], sel).astype(BF16) for j in range(W // HD)], axis=1))
    xe = jnp.concatenate(spread, axis=0)
    ins[2].wait()
    kk = dot(xe, wk_s[...])
    ins[3].wait()
    vv = dot(xe, wv_s[...])
    for hd in range(2):
        part[:, (NH + hd) * HD:(NH + hd + 1) * HD] = kk[hd * ROWS:(hd + 1) * ROWS]
        part[:, (NH + 2 + hd) * HD:(NH + 3 + hd) * HD] = vv[hd * ROWS:(hd + 1) * ROWS]
    ins[4].wait()
    for hd in range(NH):
        part[:, hd * HD:(hd + 1) * HD] = dot(x, wq_s[hd])
    pl.semaphore_wait(barrier, NZ - 1)
    copies = []
    for k, p in enumerate(peers):
        c = pltpu.make_async_remote_copy(
            src_ref=part.at[pl.ds(pl.multiple_of(p * RB, RB), RB)], dst_ref=recv.at[k], send_sem=send_sem.at[k], recv_sem=recv_sem.at[k],
            device_id={'dm': p}, device_id_type=MESH)
        c.start()
        copies.append(c)
    ins[5].wait()
    ins[6].wait()
    own = part[pl.ds(pl.multiple_of(z * RB, RB), RB), :]
    for c in copies:
        c.wait_recv()
    parts = [own] + [recv[k] for k in range(NZ - 1)]
    stats = [t[:, QKV:PAY] for t in parts]
    glob = lax.rsqrt((stats[0] + stats[1] + stats[2] + stats[3]) / (NZ * W) + EPS)
    ratio = [glob * jnp.sqrt(s / W + EPS) for s in stats]

    def head(i):
        cols = slice(i * HD, (i + 1) * HD)
        return sum(t[:, cols] * r for t, r in zip(parts, ratio))

    cs = jnp.concatenate([cos_s[...], cos_s[...]], axis=1)
    sn = jnp.concatenate([-sin_s[...], sin_s[...]], axis=1)

    def rope(t):
        return (t * cs + pltpu.roll(t, HD // 2, 1) * sn).astype(BF16).astype(F32)

    for i in range(NH):
        q_o[:, i, :] = rope(head(i))
    for i in range(NH, 8):
        q_o[:, i, :] = jnp.zeros((RB, HD), F32)
    for hd in range(2):
        kn = rope(head(NH + hd))
        vn = head(NH + 2 + hd).astype(BF16).astype(F32)
        for r in range(hd, 8, 2):
            k_o[:, r, :] = kn
            v_o[:, r, :] = vn
    for c in copies:
        c.wait_send()
    for c in caches:
        c.wait()


def attn_kernel(lens, q, kn, vn, kc, vc, o, k_out, v_out, kc_a, vc_a, o_s, sem):
    del kc, vc
    r16 = lax.broadcasted_iota(jnp.int32, (16, HD), 0)
    writes = []
    for b in range(RB):
        ln = lens[b]
        base = pl.multiple_of(b * SEQ2 + (ln // 8) * 16, 16)
        hit = (r16 // 2) == (ln % 8)
        for j, (new, cache, out) in enumerate(((kn, kc_a, k_out), (vn, vc_a, v_out))):
            fresh = jnp.concatenate([new[b], new[b]], axis=0)
            tile = cache[pl.ds(base, 16), :].astype(F32)
            cache[pl.ds(base, 16), :] = jnp.where(hit, fresh, tile).astype(BF16)
            rows = pl.ds(b * SEQ2, SEQ2)
            w = pltpu.make_async_copy(cache.at[rows], out.at[rows], sem.at[j, b])
            w.start()
            writes.append(w)
    row = lax.broadcasted_iota(jnp.int32, (16, SEQ2), 0)
    col = lax.broadcasted_iota(jnp.int32, (16, SEQ2), 1)
    same_head = (col % 2) == jnp.where(row % 8 < GRP, 0, 1)
    slot = jnp.where(same_head, col // 2, SEQ2)
    zero = jnp.zeros((8, HD), F32)
    row1 = lax.broadcasted_iota(jnp.int32, (16, 1), 0)
    for b in range(0, RB, 2):
        lhs = jnp.concatenate([jnp.concatenate([q[b], zero], axis=1),
                               jnp.concatenate([zero, q[b + 1]], axis=1)], axis=0).astype(BF16)
        r0, r1 = pl.ds(b * SEQ2, SEQ2), pl.ds((b + 1) * SEQ2, SEQ2)
        kk = jnp.concatenate([kc_a[r0, :], kc_a[r1, :]], axis=1)
        s = lax.dot_general(lhs, kk, (((1,), (1,)), ((), ())), preferred_element_type=F32)
        ln = jnp.where(row1 < 8, lens[b], lens[b + 1])
        s = jnp.where(slot <= ln, s * (HD ** -0.5), -1e30)
        e = jnp.exp(s - jnp.max(s, axis=1, keepdims=True))
        pr = (e * (1.0 / jnp.sum(e, axis=1, keepdims=True))).astype(BF16)
        vv = jnp.concatenate([vc_a[r0, :], vc_a[r1, :]], axis=1)
        oo = dot(pr, vv)
        o_s[b] = oo[:8, :HD]
        o_s[b + 1] = oo[8:, HD:]
    for hd in range(NH):
        o[:, hd * HD:(hd + 1) * HD] = o_s[:, hd, :].astype(BF16)
    for w in writes:
        w.wait()


def tail_kernel(o, hid, gain, w_o, w_g, w_u, w_d, out,
                o_all, h_s, g_s, wo_s, wg_s, wu_s, wd_s, part, rs_recv, h1_all, st_send, st_recv,
                nsend, fsend, nrecv, frecv, m_all, part2, rs2_recv, ho_all,
                w_sem, o_send, o_recv, rs_send, rs_rcv, h1_send, h1_recv, st_ss, st_rs,
                ns_sem, fs_sem, nr_sem, fr_sem, m_send, m_recv, rs2_send, rs2_rcv, ho_send, ho_recv):
    z = lax.axis_index('dm')
    t = lax.axis_index('tp')
    zp, tp = partners(z), partners(t)
    loads = [pltpu.make_async_copy(s, d, w_sem.at[i]) for i, (s, d) in enumerate(
        ((w_o, wo_s), (hid, h_s), (gain, g_s), (w_g, wg_s), (w_u, wu_s), (w_d, wd_s)))]
    for c in loads:
        c.start()
    barrier = pltpu.get_barrier_semaphore()
    for p in zp:
        pl.semaphore_signal(barrier, inc=1, device_id={'dm': p}, device_id_type=MESH)
    for p in tp:
        pl.semaphore_signal(barrier, inc=1, device_id={'tp': p}, device_id_type=MESH)
    pl.semaphore_wait(barrier, 6)

    def remote(src, dst, ss, rs, dev):
        c = pltpu.make_async_remote_copy(src_ref=src, dst_ref=dst, send_sem=ss, recv_sem=rs, device_id=dev, device_id_type=MESH)
        c.start()
        return c

    def my(i):
        return pl.ds(pl.multiple_of(i * RB, RB), RB)

    pending = []
    cps = [remote(o, o_all.at[k], o_send.at[k], o_recv.at[k], {'dm': p}) for k, p in enumerate(zp)]
    pending += cps
    loads[0].wait()
    part[my(z), :] = dot(o[...], wo_s[...])
    for k in (2, 1, 0):
        cps[k].wait_recv()
        part[my(zp[k]), :] = dot(o_all[k], wo_s[...])

    def tp_scatter(buf, recv, ss, rs):
        cs = [remote(buf.at[my(p)], recv.at[k], ss.at[k], rs.at[k], {'tp': p}) for k, p in enumerate(tp)]
        tot = buf[my(t), :]
        for k in (2, 1, 0):
            cs[k].wait_recv()
            tot = tot + recv[k]
        pending.extend(cs)
        return tot

    def tp_gather(buf, ss, rs):
        cs = [remote(buf.at[my(t)], buf.at[my(t)], ss.at[k], rs.at[k], {'tp': p}) for k, p in enumerate(tp)]
        for c in cs:
            c.wait_recv()
        pending.extend(cs)

    tot = tp_scatter(part, rs_recv, rs_send, rs_rcv)
    loads[1].wait()
    h1 = (h_s[my(t), :].astype(F32) + tot.astype(BF16).astype(F32)).astype(BF16)
    h1_all[my(t), :] = h1
    tp_gather(h1_all, h1_send, h1_recv)
    hf = h1_all[...].astype(F32)
    ss, scale = local_scale(hf, W)
    ssb = jnp.broadcast_to(ss, (ROWS, HD))
    st_send[...] = jnp.transpose(ssb)[:8, :]
    scp = [remote(st_send, st_recv.at[k], st_ss.at[k], st_rs.at[k], {'dm': p}) for k, p in enumerate(zp)]
    pending += scp
    loads[2].wait()
    x2 = (hf * scale * g_s[...].astype(F32).reshape(1, W)).astype(BF16)
    loads[3].wait()
    loads[4].wait()

    nd = z // 2
    end = (z % 3) == 0
    mid = jnp.logical_not(end)
    step = 1 - 2 * nd
    near_dst, far_dst = z + step, z - step
    near_ok, far_ok = {'dm': lax.rem(near_dst + NZ, NZ)}, {'dm': lax.rem(far_dst + NZ, NZ)}

    def piece(c):
        cols = pl.ds(pl.multiple_of(c * PC, PC), PC)
        return dot(x2, jnp.concatenate([wg_s[:, cols], wu_s[:, cols]], axis=1))

    def near_copy(i, dst, rsem):
        return pltpu.make_async_remote_copy(src_ref=nsend.at[i], dst_ref=dst.at[i], send_sem=ns_sem.at[i], recv_sem=rsem.at[i],
                                            device_id=near_ok, device_id_type=MESH)

    def far_copy(i):
        return pltpu.make_async_remote_copy(src_ref=fsend.at[i], dst_ref=frecv.at[i], send_sem=fs_sem.at[i], recv_sem=fr_sem.at[i],
                                            device_id=far_ok, device_id_type=MESH)

    def m_copies(i):
        cb = (1 - nd) * NP + i
        return [pltpu.make_async_remote_copy(src_ref=m_all.at[cb], dst_ref=m_all.at[cb], send_sem=m_send.at[k, i], recv_sem=m_recv.at[cb],
                                             device_id={'dm': p}, device_id_type=MESH) for k, p in enumerate(zp)]

    @pl.when(end)
    def _():
        for i in range(NP):
            nsend[i] = piece(nd * NP + i)
            near_copy(i, nrecv, nr_sem).start()

    for c in scp:
        c.wait_recv()

    def col(row8):
        return jnp.transpose(jnp.broadcast_to(row8[0:1, :], (HD, ROWS)))

    sts = [col(st_recv[k]) for k in range(NZ - 1)]
    glob = lax.rsqrt((ssb + sts[0] + sts[1] + sts[2]) / (NZ * W) + EPS)
    r_me = glob * jnp.sqrt(ssb / W + EPS)
    r_end = glob * jnp.sqrt(sts[2] / W + EPS)
    r_me2 = jnp.concatenate([r_me, r_me], axis=1)
    r_end2 = jnp.concatenate([r_end, r_end], axis=1)

    @pl.when(mid)
    def _():
        def near(i):
            mine = piece(nd * NP + i) * r_me2
            near_copy(i, nrecv, nr_sem).wait_recv()
            nsend[i] = nrecv[i] * r_end2 + mine
            near_copy(i, frecv, fr_sem).start()

        def far(i):
            mine = piece((1 - nd) * NP + i) * r_me2
            far_copy(i).wait_recv()
            fsend[i] = frecv[i] + mine
            far_copy(i).start()

        for i in range(NP + 2):
            if i < NP:
                near(i)
            if i >= 2:
                far(i - 2)

    @pl.when(end)
    def _():
        for i in range(NP):
            mine = piece((1 - nd) * NP + i) * r_me2
            far_copy(i).wait_recv()
            tot = frecv[i] + mine
            gate, up = tot[:, :PC], tot[:, PC:]
            m_all[(1 - nd) * NP + i] = (gate * (1.0 / (1.0 + jnp.exp(-gate))) * up).astype(BF16)
            for c in m_copies(i):
                c.start()

    def m_wait(cb, i):
        pltpu.make_async_remote_copy(src_ref=m_all.at[cb], dst_ref=m_all.at[cb], send_sem=m_send.at[0, i], recv_sem=m_recv.at[cb],
                                     device_id={'dm': zp[0]}, device_id_type=MESH).wait_recv()

    loads[5].wait()
    for i in range(NP):
        m_wait(nd * NP + i, i)

        @pl.when(mid)
        def _():
            m_wait((1 - nd) * NP + i, i)

    acc = None
    for j in range(NP):
        d = dot(jnp.concatenate([m_all[2 * j], m_all[2 * j + 1]], axis=1), wd_s[2 * j * PC:2 * (j + 1) * PC, :])
        acc = d if acc is None else acc + d
    part2[...] = acc
    tot = tp_scatter(part2, rs2_recv, rs2_send, rs2_rcv)
    ho_all[my(t), :] = (h1_all[my(t), :].astype(F32) + tot.astype(BF16).astype(F32)).astype(BF16)
    tp_gather(ho_all, ho_send, ho_recv)
    out[...] = ho_all[...]
    for c in pending:
        c.wait_send()

    @pl.when(end)
    def _():
        for i in range(NP):
            near_copy(i, nrecv, nr_sem).wait_send()
            for c in m_copies(i):
                c.wait_send()

    @pl.when(mid)
    def _():
        for i in range(NP):
            near_copy(i, frecv, fr_sem).wait_send()
            far_copy(i).wait_send()


def local_layer(hidden, w_q, w_k, w_v, w_o, w_gate, w_up, w_down, norm_attn, norm_mlp, k_cache, v_cache, seq_lens, rope_cos, rope_sin):
    mib = 1 << 20
    kc = k_cache.reshape(RB * SEQ2, HD)
    vc = v_cache.reshape(RB * SEQ2, HD)
    q, kn, vn, kc, vc = pl.pallas_call(
        qkv_kernel,
        out_shape=(pltpu.VMEM((RB, 8, HD), F32), pltpu.VMEM((RB, 8, HD), F32), pltpu.VMEM((RB, 8, HD), F32),
                   pltpu.VMEM((RB * SEQ2, HD), BF16), pltpu.VMEM((RB * SEQ2, HD), BF16)),
        in_specs=[ANY] * 9,
        out_specs=(VM,) * 5,
        scratch_shapes=[
            pltpu.VMEM((ROWS, W), BF16), pltpu.VMEM((W,), BF16), pltpu.VMEM((NH, W, HD), BF16),
            pltpu.VMEM((2 * W, HD), BF16), pltpu.VMEM((2 * W, HD), BF16), pltpu.VMEM((RB, HD // 2), F32), pltpu.VMEM((RB, HD // 2), F32),
            pltpu.VMEM((ROWS, PAY), F32), pltpu.VMEM((NZ - 1, RB, PAY), F32),
            DMA((7,)), DMA((2,)), DMA((3,)), DMA((3,))],
        compiler_params=pltpu.CompilerParams(collective_id=0, has_side_effects=True, vmem_limit_bytes=40 * mib),
        name='qkv',
    )(hidden, norm_attn, w_q.transpose(1, 0, 2), w_k.reshape(2 * W, HD), w_v.reshape(2 * W, HD), rope_cos, rope_sin, kc, vc)

    o, k_out, v_out, _, _ = pl.pallas_call(
        attn_kernel,
        out_shape=(pltpu.VMEM((RB, W), BF16), jax.ShapeDtypeStruct((RB * SEQ2, HD), BF16), jax.ShapeDtypeStruct((RB * SEQ2, HD), BF16),
                   pltpu.VMEM((RB * SEQ2, HD), BF16), pltpu.VMEM((RB * SEQ2, HD), BF16)),
        in_specs=[SM, VM, VM, VM, VM, VM],
        out_specs=(VM, ANY, ANY, VM, VM),
        scratch_shapes=[pltpu.VMEM((RB, 8, HD), F32), DMA((2, RB))],
        input_output_aliases={4: 3, 5: 4},
        compiler_params=pltpu.CompilerParams(vmem_limit_bytes=40 * mib),
        name='attn',
    )(seq_lens, q, kn, vn, kc, vc)

    h_out = pl.pallas_call(
        tail_kernel,
        out_shape=jax.ShapeDtypeStruct((ROWS, W), BF16),
        in_specs=[VM] + [ANY] * 6,
        out_specs=VM,
        scratch_shapes=[
            pltpu.VMEM((NZ - 1, RB, W), BF16), pltpu.VMEM((ROWS, W), BF16), pltpu.VMEM((W,), BF16),
            pltpu.VMEM((W, W), BF16), pltpu.VMEM((W, FFL), BF16), pltpu.VMEM((W, FFL), BF16), pltpu.VMEM((FFL, W), BF16),
            pltpu.VMEM((ROWS, W), F32), pltpu.VMEM((NT - 1, RB, W), F32), pltpu.VMEM((ROWS, W), BF16),
            pltpu.VMEM((8, ROWS), F32), pltpu.VMEM((NZ - 1, 8, ROWS), F32),
            pltpu.VMEM((NP, ROWS, 2 * PC), F32), pltpu.VMEM((NP, ROWS, 2 * PC), F32), pltpu.VMEM((NP, ROWS, 2 * PC), F32),
            pltpu.VMEM((NP, ROWS, 2 * PC), F32), pltpu.VMEM((2 * NP, ROWS, PC), BF16),
            pltpu.VMEM((ROWS, W), F32), pltpu.VMEM((NT - 1, RB, W), F32), pltpu.VMEM((ROWS, W), BF16),
            DMA((6,)), DMA((3,)), DMA((3,)), DMA((3,)), DMA((3,)), DMA((3,)), DMA((3,)), DMA((3,)), DMA((3,)),
            DMA((NP,)), DMA((NP,)), DMA((NP,)), DMA((NP,)), DMA((3, NP)), DMA((2 * NP,)), DMA((3,)), DMA((3,)), DMA((3,)), DMA((3,))],
        compiler_params=pltpu.CompilerParams(collective_id=1, has_side_effects=True, vmem_limit_bytes=40 * mib),
        name='tail',
    )(o, hidden, norm_mlp, w_o.reshape(W, W), w_gate, w_up, w_down)
    shape = (RB, SEQ2 // 2, 2, HD)
    return h_out, k_out.reshape(shape), v_out.reshape(shape)


def solution(mesh):
    row_spec = P('dp', 'dm')
    cache_spec = P(('dp', 'dm'), None, 'tp', None)
    batch_spec = P(('dp', 'dm'))
    rope_spec = P(('dp', 'dm'), None)
    in_specs = (row_spec, P('dm', 'tp', None), P('dm', 'tp', None), P('dm', 'tp', None), P('tp', None, 'dm'), P('dm', 'tp'), P('dm', 'tp'), P('tp', 'dm'), P('dm'), P('dm'), cache_spec, cache_spec, batch_spec, rope_spec, rope_spec)
    return jax.shard_map(local_layer, mesh=mesh, in_specs=in_specs, out_specs=(row_spec, cache_spec, cache_spec), check_vma=False)
```

time: 220 us -> 91 us (0.41)
  waiting for transfers between devices: 83 us -> 0 us
  Pallas kernels: 0 us -> 72.1 us
  blocking collectives: 61.9 us -> 0 us
  other arithmetic: 33.9 us -> 0 us
  matrix products: 26 us -> 0 us
  local copies, waits for them, and re-layouts: 0.09 us -> 18 us
  between operations: 13.9 us -> 0.73 us
    pallas_call x0 -> x3, Pallas kernels: none -> 72.1 us  [the longest x1 49.2 us: local_layer(): pl.pallas_call(tail_kernel, out_shape=jax.ShapeDtypeStruct((ROWS, W), BF1...]
    psum x1 -> x0, waiting for transfers between devices: 51.9 us -> none  [local_layer(): lax.psum(jnp.dot(x_mlp, w_up, preferred_element_type=jnp.float32), 'dm')]
    psum x4 -> x0, blocking collectives: 48.7 us -> none  [the longest x2 22.4 us: width_norm(): sq_sum = lax.psum(jnp.sum(x_f32 * x_f32, axis=-1, keepdims=True), 'dm')]
    reduce_scatter x3 -> x0, waiting for transfers between devices: 31 us -> none  [the longest x1 19.3 us: local_layer(): v_rows = lax.psum_scatter(v_part, 'dm', scatter_dimension=0, tiled=True)]
    select_n x1 -> x0, other arithmetic: 26.3 us -> none  [attend(): k_out = jnp.where(write_mask, k_rot[:, None], k_cache)]
    dot_general x8 -> x0, matrix products: 19.4 us -> none  [the longest x1 5.03 us: attend(): jnp.einsum('bkgs,bskd->bkgd', attn_probs, v_out, preferred_element_type=j...]
    unnamed x10 -> x27, local copies, waits for them, and re-layouts: 0.03 us -> 18 us
    all_gather x1 -> x0, blocking collectives: 13.2 us -> none  [local_layer(): heads_all = lax.all_gather(attn_heads, 'dm', axis=0, tiled=True)]
  transfers between devices with their start and end apart: 4 -> 0, of which waited for: 3 -> 0; matrix products, arithmetic and copies ran while one was open for 15% -> 0% of each run, Pallas kernels for 0% -> 0%
where the time goes in v1:
time: 91 us; the launch traced here: 90.8 us
  Pallas kernels  72.1 us (79%)
  local copies, waits for them, and re-layouts  18 us (20%)
    pallas_call x1, Pallas kernels, local_layer(): pl.pallas_call(tail_kernel, out_shape=jax.ShapeDtypeStruct((ROWS, W), BF1...  49.2 us
    unnamed x27, local copies, waits for them, and re-layouts  18 us
    pallas_call x1, Pallas kernels, local_layer(): pl.pallas_call(qkv_kernel, out_shape=(pltpu.VMEM((RB, 8, HD), F32), pltpu...  14.9 us
    pallas_call x1, Pallas kernels, local_layer(): pl.pallas_call(attn_kernel, out_shape=(pltpu.VMEM((RB, W), BF16), jax.Sha...  8.01 us

profile of v1, /device:TPU:0, one launch (start us, length us, event | category | flops | bytes accessed | tf_op | source)
XLA Modules:
  0.0 90.8 jit_solution(1446894747706472413)
XLA Ops:
  0.6 14.9 %qkv.1 = (f32[16,8,128]{2,1,0:T(8,128)S(1)}, f32[16,8,128]{2,1,0:T(8,128)S(1)}, f32[16,8,128]{2,1,0:T(8,128)S(1)}, bf16[32768,128]{1,0:T(8,128)(2,1)S(1)}, bf16[32768,128]{1,0:T(8,128)(2,1)S(1)}) custom-call(bf16[64,768]{1,0:T(8,128)(2,1)} %hid.3, bf16[768]{0:T(1024)(128)(2,1)} %gain.2, bf16[6,768,128]{2,1,0:T(8,128)(2,1)} %bitcast.11, ...), custom_call_target="tpu_custom_call" | custom-call | tf_op jit(solution)/shard_map/qkv/pallas_call | solution.py:356
  15.5 0.0 copy-start
  15.5 3.4 %copy-done = bf16[32768,128]{1,0:T(8,128)(2,1)} copy-done((bf16[32768,128]{1,0:T(8,128)(2,1)}, bf16[32768,128]{1,0:T(8,128)(2,1)S(1)}, u32[]{:S(2)}) %copy-start) | copy-done | bytes 8388632
  18.9 0.0 copy-start.2
  18.9 3.4 %copy-done.2 = bf16[32768,128]{1,0:T(8,128)(2,1)} copy-done((bf16[32768,128]{1,0:T(8,128)(2,1)}, bf16[32768,128]{1,0:T(8,128)(2,1)S(1)}, u32[]{:S(2)}) %copy-start.2) | copy-done | bytes 8388632
  22.3 0.0 copy-start.9
  22.3 0.6 copy-done.9
  22.9 0.0 copy-start.10
  22.9 0.6 copy-done.10
  23.6 0.0 copy-start.11
  23.6 0.6 copy-done.11
  24.2 0.0 copy-start.1
  24.2 3.4 %copy-done.1 = bf16[32768,128]{1,0:T(8,128)(2,1)S(1)} copy-done((bf16[32768,128]{1,0:T(8,128)(2,1)S(1)}, bf16[32768,128]{1,0:T(8,128)(2,1)}, u32[]{:S(2)}) %copy-start.1) | copy-done | bytes 8388632
  27.6 0.0 copy-start.3
  27.6 3.4 %copy-done.3 = bf16[32768,128]{1,0:T(8,128)(2,1)S(1)} copy-done((bf16[32768,128]{1,0:T(8,128)(2,1)S(1)}, bf16[32768,128]{1,0:T(8,128)(2,1)}, u32[]{:S(2)}) %copy-start.3) | copy-done | bytes 8388632
  31.0 0.0 copy-start.4
  31.0 0.0 copy-start.5
  31.0 0.0 copy-start.7
  31.0 0.0 copy-start.8
  31.0 0.0 copy-start.12
  31.0 8.0 %attn.1 = (bf16[16,768]{1,0:T(8,128)(2,1)S(1)}, bf16[32768,128]{1,0:T(8,128)(2,1)}, bf16[32768,128]{1,0:T(8,128)(2,1)}, bf16[32768,128]{1,0:T(8,128)(2,1)S(1)}, bf16[32768,128]{1,0:T(8,128)(2,1)S(1)}) custom-call(s32[16]{0:T(128)} %lens.1, f32[16,8,128]{2,1,0:T(8,128)} %copy-done.9, ...), custom_call_target="tpu_custom_call", output_to_operand_aliasing={{3}: (4, {}), {4}: (5, {})} | custom-call | tf_op jit(solution)/shard_map/attn/pallas_call | solution.py:371
  39.0 0.0 copy-done.4
  39.0 0.0 copy-done.5
  39.0 0.0 copy-done.7
  39.0 0.0 copy-done.8
  39.0 0.0 copy-done.12
  39.1 0.0 copy-start.6
  39.1 1.9 %copy-done.6 = bf16[2048,768]{1,0:T(8,128)(2,1)S(1)} copy-done((bf16[2048,768]{1,0:T(8,128)(2,1)S(1)}, bf16[2048,768]{1,0:T(8,128)(2,1)}, u32[]{:S(2)}) %copy-start.6) | copy-done | bytes 3145752
  40.9 49.2 %tail.1 = bf16[64,768]{1,0:T(8,128)(2,1)S(1)} custom-call(bf16[16,768]{1,0:T(8,128)(2,1)S(1)} %get-tuple-element.16.o, bf16[64,768]{1,0:T(8,128)(2,1)S(1)} %copy-done.8, bf16[768]{0:T(1024)(128)(2,1)S(1)} %copy-done.12, bf16[768,768]{1,0:T(8,128)(2,1)S(1)} %bitcast.8, bf16[768,2048]{1,0:T(8,128)(2,1)S(1)} %copy-done.4, bf16[768,2048]{1,0:T(8,128)(2,1)S(1)} %copy-done.5, ...), custom_call_target="tpu_custom_call" | custom-call | tf_op jit(solution)/shard_map/tail/pallas_call | solution.py:383
  90.1 0.6 copy.23
Async XLA Ops:
  15.5 3.4 %copy-start = (bf16[32768,128]{1,0:T(8,128)(2,1)}, bf16[32768,128]{1,0:T(8,128)(2,1)S(1)}, u32[]{:S(2)}) copy-start(bf16[32768,128]{1,0:T(8,128)(2,1)S(1)} %get-tuple-element.14.kc) | copy-start | bytes 25165828
  18.9 3.4 %copy-start.2 = (bf16[32768,128]{1,0:T(8,128)(2,1)}, bf16[32768,128]{1,0:T(8,128)(2,1)S(1)}, u32[]{:S(2)}) copy-start(bf16[32768,128]{1,0:T(8,128)(2,1)S(1)} %get-tuple-element.15.vc) | copy-start | bytes 25165828
  22.3 0.6 copy-start.9
  22.9 0.6 copy-start.10
  23.6 0.6 copy-start.11
  24.2 3.4 %copy-start.1 = (bf16[32768,128]{1,0:T(8,128)(2,1)S(1)}, bf16[32768,128]{1,0:T(8,128)(2,1)}, u32[]{:S(2)}) copy-start(bf16[32768,128]{1,0:T(8,128)(2,1)} %copy-done) | copy-start | bytes 25165828
  27.6 3.4 %copy-start.3 = (bf16[32768,128]{1,0:T(8,128)(2,1)S(1)}, bf16[32768,128]{1,0:T(8,128)(2,1)}, u32[]{:S(2)}) copy-start(bf16[32768,128]{1,0:T(8,128)(2,1)} %copy-done.2) | copy-start | bytes 25165828
  31.0 8.0 %copy-start.4 = (bf16[768,2048]{1,0:T(8,128)(2,1)S(1)}, bf16[768,2048]{1,0:T(8,128)(2,1)}, u32[]{:S(2)}) copy-start(bf16[768,2048]{1,0:T(8,128)(2,1)} %w_g.1) | copy-start | bytes 9437188
  31.0 8.1 %copy-start.5 = (bf16[768,2048]{1,0:T(8,128)(2,1)S(1)}, bf16[768,2048]{1,0:T(8,128)(2,1)}, u32[]{:S(2)}) copy-start(bf16[768,2048]{1,0:T(8,128)(2,1)} %w_u.1) | copy-start | bytes 9437188
  31.0 8.1 %copy-start.7 = (bf16[6,128,768]{2,1,0:T(8,128)(2,1)S(1)}, bf16[6,128,768]{2,1,0:T(8,128)(2,1)}, u32[]{:S(2)}) copy-start(bf16[6,128,768]{2,1,0:T(8,128)(2,1)} %param.19) | copy-start | bytes 3538948
  31.0 8.1 %copy-start.8 = (bf16[64,768]{1,0:T(8,128)(2,1)S(1)}, bf16[64,768]{1,0:T(8,128)(2,1)}, u32[]{:S(2)}) copy-start(bf16[64,768]{1,0:T(8,128)(2,1)} %hid.3) | copy-start | bytes 294916
  31.0 8.1 %copy-start.12 = (bf16[768]{0:T(1024)(128)(2,1)S(1)}, bf16[768]{0:T(1024)(128)(2,1)}, u32[]{:S(2)}) copy-start(bf16[768]{0:T(1024)(128)(2,1)} %gain.3) | copy-start | bytes 4612
  39.1 1.9 %copy-start.6 = (bf16[2048,768]{1,0:T(8,128)(2,1)S(1)}, bf16[2048,768]{1,0:T(8,128)(2,1)}, u32[]{:S(2)}) copy-start(bf16[2048,768]{1,0:T(8,128)(2,1)} %w_d.1) | copy-start | bytes 9437188

commit v2 on v1

--- a/solution.py
+++ b/solution.py
@@ -351,8 +351,13 @@
 
 def local_layer(hidden, w_q, w_k, w_v, w_o, w_gate, w_up, w_down, norm_attn, norm_mlp, k_cache, v_cache, seq_lens, rope_cos, rope_sin):
     mib = 1 << 20
-    kc = k_cache.reshape(RB * SEQ2, HD)
-    vc = v_cache.reshape(RB * SEQ2, HD)
+
+    def hbm(*arrays):
+        return [pltpu.with_memory_space_constraint(a, pltpu.HBM) for a in arrays]
+
+    def vmem(*arrays):
+        return [pltpu.with_memory_space_constraint(a, pltpu.VMEM) for a in arrays]
+
     q, kn, vn, kc, vc = pl.pallas_call(
         qkv_kernel,
         out_shape=(pltpu.VMEM((RB, 8, HD), F32), pltpu.VMEM((RB, 8, HD), F32), pltpu.VMEM((RB, 8, HD), F32),
@@ -366,7 +371,8 @@
             DMA((7,)), DMA((2,)), DMA((3,)), DMA((3,))],
         compiler_params=pltpu.CompilerParams(collective_id=0, has_side_effects=True, vmem_limit_bytes=40 * mib),
         name='qkv',
-    )(hidden, norm_attn, w_q.transpose(1, 0, 2), w_k.reshape(2 * W, HD), w_v.reshape(2 * W, HD), rope_cos, rope_sin, kc, vc)
+    )(*hbm(hidden, norm_attn, w_q.transpose(1, 0, 2), w_k.reshape(2 * W, HD), w_v.reshape(2 * W, HD), rope_cos, rope_sin,
+           k_cache.reshape(RB * SEQ2, HD), v_cache.reshape(RB * SEQ2, HD)))
 
     o, k_out, v_out, _, _ = pl.pallas_call(
         attn_kernel,
@@ -378,7 +384,7 @@
         input_output_aliases={4: 3, 5: 4},
         compiler_params=pltpu.CompilerParams(vmem_limit_bytes=40 * mib),
         name='attn',
-    )(seq_lens, q, kn, vn, kc, vc)
+    )(seq_lens, *vmem(q, kn, vn, kc, vc))
 
     h_out = pl.pallas_call(
         tail_kernel,
@@ -397,7 +403,7 @@
             DMA((NP,)), DMA((NP,)), DMA((NP,)), DMA((NP,)), DMA((3, NP)), DMA((2 * NP,)), DMA((3,)), DMA((3,)), DMA((3,)), DMA((3,))],
         compiler_params=pltpu.CompilerParams(collective_id=1, has_side_effects=True, vmem_limit_bytes=40 * mib),
         name='tail',
-    )(o, hidden, norm_mlp, w_o.reshape(W, W), w_gate, w_up, w_down)
+    )(*vmem(o), *hbm(hidden, norm_mlp, w_o.reshape(W, W), w_gate, w_up, w_down))
     shape = (RB, SEQ2 // 2, 2, HD)
     return h_out, k_out.reshape(shape), v_out.reshape(shape)
 

time: 91 us -> 71.8 us (0.79)
  local copies, waits for them, and re-layouts: 18 us -> 0.64 us
  Pallas kernels: 72.1 us -> 70.3 us
    unnamed x27 -> x1, local copies, waits for them, and re-layouts: 18 us -> 0.64 us
    pallas_call x1, Pallas kernels: 49.2 us -> 48.2 us  [local_layer(): pl.pallas_call(tail_kernel, out_shape=jax.ShapeDtypeStruct((ROWS, W), BF1...]
where the time goes in v2:
time: 71.8 us; the launch traced here: 71.6 us
  Pallas kernels  70.3 us (98%)
    pallas_call x1, Pallas kernels, local_layer(): pl.pallas_call(tail_kernel, out_shape=jax.ShapeDtypeStruct((ROWS, W), BF1...  48.2 us
    pallas_call x1, Pallas kernels, local_layer(): pl.pallas_call(qkv_kernel, out_shape=(pltpu.VMEM((RB, 8, HD), F32), pltpu...  14.9 us
    pallas_call x1, Pallas kernels, local_layer(): pl.pallas_call(attn_kernel, out_shape=(pltpu.VMEM((RB, W), BF16), jax.Sha...  7.19 us

profile of v2, /device:TPU:0, one launch (start us, length us, event | category | flops | bytes accessed | tf_op | source)
XLA Modules:
  0.0 71.6 jit_solution(4663930609373430762)
XLA Ops:
  0.6 14.9 %qkv.1 = (f32[16,8,128]{2,1,0:T(8,128)S(1)}, f32[16,8,128]{2,1,0:T(8,128)S(1)}, f32[16,8,128]{2,1,0:T(8,128)S(1)}, bf16[32768,128]{1,0:T(8,128)(2,1)S(1)}, bf16[32768,128]{1,0:T(8,128)(2,1)S(1)}) custom-call(bf16[64,768]{1,0:T(8,128)(2,1)} %hid.3, bf16[768]{0:T(1024)(128)(2,1)} %gain.2, bf16[6,768,128]{2,1,0:T(8,128)(2,1)} %bitcast.10, ...), custom_call_target="tpu_custom_call" | custom-call | tf_op jit(solution)/shard_map/qkv/pallas_call | solution.py:361
  15.5 7.2 %attn.1 = (bf16[16,768]{1,0:T(8,128)(2,1)S(1)}, bf16[32768,128]{1,0:T(8,128)(2,1)}, bf16[32768,128]{1,0:T(8,128)(2,1)}, bf16[32768,128]{1,0:T(8,128)(2,1)S(1)}, bf16[32768,128]{1,0:T(8,128)(2,1)S(1)}) custom-call(s32[16]{0:T(128)} %lens.1, f32[16,8,128]{2,1,0:T(8,128)S(1)} %get-tuple-element.11.q, ...), custom_call_target="tpu_custom_call", output_to_operand_aliasing={{3}: (4, {}), {4}: (5, {})} | custom-call | tf_op jit(solution)/shard_map/attn/pallas_call | solution.py:377
  22.7 48.2 %tail.1 = bf16[64,768]{1,0:T(8,128)(2,1)S(1)} custom-call(bf16[16,768]{1,0:T(8,128)(2,1)S(1)} %get-tuple-element.16.o, bf16[64,768]{1,0:T(8,128)(2,1)} %hid.3, bf16[768]{0:T(1024)(128)(2,1)} %gain.3, bf16[768,768]{1,0:T(8,128)(2,1)} %bitcast.11, bf16[768,2048]{1,0:T(8,128)(2,1)} %w_g.1, bf16[768,2048]{1,0:T(8,128)(2,1)} %w_u.1, bf16[2048,768]{1,0:T(8,128)(2,1)} %w_d.1), custom_call_target="tpu_custom_call" | custom-call | tf_op jit(solution)/shard_map/tail/pallas_call | solution.py:389
  71.0 0.6 copy.23

commit v3 on v2

--- a/solution.py
+++ b/solution.py
@@ -28,6 +28,8 @@
 FFL = 2048
 NP = 8
 PC = 128
+NS = 2
+SUB = ROWS // NS
 
 
 def partners(i):
@@ -128,56 +130,29 @@
         c.wait()
 
 
-def attn_kernel(lens, q, kn, vn, kc, vc, o, k_out, v_out, kc_a, vc_a, o_s, sem):
+def patch_kernel(lens, kn, vn, kc, vc, kc_a, vc_a):
     del kc, vc
     r16 = lax.broadcasted_iota(jnp.int32, (16, HD), 0)
-    writes = []
     for b in range(RB):
         ln = lens[b]
         base = pl.multiple_of(b * SEQ2 + (ln // 8) * 16, 16)
         hit = (r16 // 2) == (ln % 8)
-        for j, (new, cache, out) in enumerate(((kn, kc_a, k_out), (vn, vc_a, v_out))):
+        for new, cache in ((kn, kc_a), (vn, vc_a)):
             fresh = jnp.concatenate([new[b], new[b]], axis=0)
             tile = cache[pl.ds(base, 16), :].astype(F32)
             cache[pl.ds(base, 16), :] = jnp.where(hit, fresh, tile).astype(BF16)
-            rows = pl.ds(b * SEQ2, SEQ2)
-            w = pltpu.make_async_copy(cache.at[rows], out.at[rows], sem.at[j, b])
-            w.start()
-            writes.append(w)
-    row = lax.broadcasted_iota(jnp.int32, (16, SEQ2), 0)
-    col = lax.broadcasted_iota(jnp.int32, (16, SEQ2), 1)
-    same_head = (col % 2) == jnp.where(row % 8 < GRP, 0, 1)
-    slot = jnp.where(same_head, col // 2, SEQ2)
-    zero = jnp.zeros((8, HD), F32)
-    row1 = lax.broadcasted_iota(jnp.int32, (16, 1), 0)
-    for b in range(0, RB, 2):
-        lhs = jnp.concatenate([jnp.concatenate([q[b], zero], axis=1),
-                               jnp.concatenate([zero, q[b + 1]], axis=1)], axis=0).astype(BF16)
-        r0, r1 = pl.ds(b * SEQ2, SEQ2), pl.ds((b + 1) * SEQ2, SEQ2)
-        kk = jnp.concatenate([kc_a[r0, :], kc_a[r1, :]], axis=1)
-        s = lax.dot_general(lhs, kk, (((1,), (1,)), ((), ())), preferred_element_type=F32)
-        ln = jnp.where(row1 < 8, lens[b], lens[b + 1])
-        s = jnp.where(slot <= ln, s * (HD ** -0.5), -1e30)
-        e = jnp.exp(s - jnp.max(s, axis=1, keepdims=True))
-        pr = (e * (1.0 / jnp.sum(e, axis=1, keepdims=True))).astype(BF16)
-        vv = jnp.concatenate([vc_a[r0, :], vc_a[r1, :]], axis=1)
-        oo = dot(pr, vv)
-        o_s[b] = oo[:8, :HD]
-        o_s[b + 1] = oo[8:, HD:]
-    for hd in range(NH):
-        o[:, hd * HD:(hd + 1) * HD] = o_s[:, hd, :].astype(BF16)
-    for w in writes:
-        w.wait()
-
-
-def tail_kernel(o, hid, gain, w_o, w_g, w_u, w_d, out,
-                o_all, h_s, g_s, wo_s, wg_s, wu_s, wd_s, part, rs_recv, h1_all, st_send, st_recv,
-                nsend, fsend, nrecv, frecv, m_all, part2, rs2_recv, ho_all,
-                w_sem, o_send, o_recv, rs_send, rs_rcv, h1_send, h1_recv, st_ss, st_rs,
-                ns_sem, fs_sem, nr_sem, fr_sem, m_send, m_recv, rs2_send, rs2_rcv, ho_send, ho_recv):
+
+
+def tail_kernel(lens, q, kc, vc, hid, gain, w_o, w_g, w_u, w_d, out,
+                o_s, o_mine, o_all, h_s, g_s, wo_s, wg_s, wu_s, wd_s, part, dd1, ys1, yr1, h1_all, st_send, st_recv,
+                nsend, fsend, nrecv, frecv, m_all, part2, dd2, ys2, yr2, ho_all,
+                w_sem, o_send, o_recv, ar1, ar2, st_ss, st_rs,
+                ns_sem, fs_sem, nr_sem, fr_sem, m_send, m_recv):
     z = lax.axis_index('dm')
     t = lax.axis_index('tp')
-    zp, tp = partners(z), partners(t)
+    zp = partners(z)
+    core = lax.rem(t, 2)
+    twin, across = t + 1 - 2 * core, lax.rem(t + 2, 4)
     loads = [pltpu.make_async_copy(s, d, w_sem.at[i]) for i, (s, d) in enumerate(
         ((w_o, wo_s), (hid, h_s), (gain, g_s), (w_g, wg_s), (w_u, wu_s), (w_d, wd_s)))]
     for c in loads:
@@ -185,9 +160,8 @@
     barrier = pltpu.get_barrier_semaphore()
     for p in zp:
         pl.semaphore_signal(barrier, inc=1, device_id={'dm': p}, device_id_type=MESH)
-    for p in tp:
+    for p in (twin, across):
         pl.semaphore_signal(barrier, inc=1, device_id={'tp': p}, device_id_type=MESH)
-    pl.semaphore_wait(barrier, 6)
 
     def remote(src, dst, ss, rs, dev):
         c = pltpu.make_async_remote_copy(src_ref=src, dst_ref=dst, send_sem=ss, recv_sem=rs, device_id=dev, device_id_type=MESH)
@@ -198,34 +172,63 @@
         return pl.ds(pl.multiple_of(i * RB, RB), RB)
 
     pending = []
-    cps = [remote(o, o_all.at[k], o_send.at[k], o_recv.at[k], {'dm': p}) for k, p in enumerate(zp)]
-    pending += cps
+    row = lax.broadcasted_iota(jnp.int32, (16, SEQ2), 0)
+    column = lax.broadcasted_iota(jnp.int32, (16, SEQ2), 1)
+    same_head = (column % 2) == jnp.where(row % 8 < GRP, 0, 1)
+    slot = jnp.where(same_head, column // 2, SEQ2)
+    zero = jnp.zeros((8, HD), F32)
+    row1 = lax.broadcasted_iota(jnp.int32, (16, 1), 0)
+    cps = []
+    for half in range(2):
+        for b in range(8 * half, 8 * half + 8, 2):
+            lhs = jnp.concatenate([jnp.concatenate([q[b], zero], axis=1),
+                                   jnp.concatenate([zero, q[b + 1]], axis=1)], axis=0).astype(BF16)
+            r0, r1 = pl.ds(b * SEQ2, SEQ2), pl.ds((b + 1) * SEQ2, SEQ2)
+            kk = jnp.concatenate([kc[r0, :], kc[r1, :]], axis=1)
+            s = lax.dot_general(lhs, kk, (((1,), (1,)), ((), ())), preferred_element_type=F32)
+            ln = jnp.where(row1 < 8, lens[b], lens[b + 1])
+            s = jnp.where(slot <= ln, s * (HD ** -0.5), -1e30)
+            e = jnp.exp(s - jnp.max(s, axis=1, keepdims=True))
+            pr = (e * (1.0 / jnp.sum(e, axis=1, keepdims=True))).astype(BF16)
+            vv = jnp.concatenate([vc[r0, :], vc[r1, :]], axis=1)
+            oo = dot(pr, vv)
+            o_s[b] = oo[:8, :HD]
+            o_s[b + 1] = oo[8:, HD:]
+        rows = pl.ds(8 * half, 8)
+        for hd in range(NH):
+            o_mine[rows, hd * HD:(hd + 1) * HD] = o_s[rows, hd, :].astype(BF16)
+        if half == 0:
+            pl.semaphore_wait(barrier, 5)
+        cps.append([remote(o_mine.at[rows], o_all.at[k, rows], o_send.at[k, half], o_recv.at[k, half], {'dm': p})
+                    for k, p in enumerate(zp)])
     loads[0].wait()
-    part[my(z), :] = dot(o[...], wo_s[...])
+    part[my(z), :] = dot(o_mine[...], wo_s[...])
     for k in (2, 1, 0):
-        cps[k].wait_recv()
+        for half in range(2):
+            cps[half][k].wait_recv()
+            pending.append(cps[half][k])
         part[my(zp[k]), :] = dot(o_all[k], wo_s[...])
 
-    def tp_scatter(buf, recv, ss, rs):
-        cs = [remote(buf.at[my(p)], recv.at[k], ss.at[k], rs.at[k], {'tp': p}) for k, p in enumerate(tp)]
-        tot = buf[my(t), :]
-        for k in (2, 1, 0):
-            cs[k].wait_recv()
-            tot = tot + recv[k]
-        pending.extend(cs)
-        return tot
-
-    def tp_gather(buf, ss, rs):
-        cs = [remote(buf.at[my(t)], buf.at[my(t)], ss.at[k], rs.at[k], {'tp': p}) for k, p in enumerate(tp)]
-        for c in cs:
+    def tp_sum(buf, base, dd, ys, yr, res, sems):
+        def rws(c, i):
+            return pl.ds(pl.multiple_of(c * 2 * RB + i * RB, RB), RB)
+        first = [remote(buf.at[rws(1 - core, i)], dd.at[i], sems.at[0, i], sems.at[1, i], {'tp': twin}) for i in range(2)]
+        second, third = [], []
+        for i in range(2):
+            first[i].wait_recv()
+            ys[i] = buf[rws(core, i), :] + dd[i]
+            second.append(remote(ys.at[i], yr.at[i], sems.at[2, i], sems.at[3, i], {'tp': across}))
+        for i in range(2):
+            second[i].wait_recv()
+            tot = ys[i] + yr[i]
+            res[rws(core, i), :] = (base[rws(core, i), :].astype(F32) + tot.astype(BF16).astype(F32)).astype(BF16)
+            third.append(remote(res.at[rws(core, i)], res.at[rws(core, i)], sems.at[4, i], sems.at[5, i], {'tp': twin}))
+        for c in third:
             c.wait_recv()
-        pending.extend(cs)
-
-    tot = tp_scatter(part, rs_recv, rs_send, rs_rcv)
+        pending.extend(first + second + third)
+
     loads[1].wait()
-    h1 = (h_s[my(t), :].astype(F32) + tot.astype(BF16).astype(F32)).astype(BF16)
-    h1_all[my(t), :] = h1
-    tp_gather(h1_all, h1_send, h1_recv)
+    tp_sum(part, h_s, dd1, ys1, yr1, h1_all, ar1)
     hf = h1_all[...].astype(F32)
     ss, scale = local_scale(hf, W)
     ssb = jnp.broadcast_to(ss, (ROWS, HD))
@@ -248,13 +251,16 @@
         cols = pl.ds(pl.multiple_of(c * PC, PC), PC)
         return dot(x2, jnp.concatenate([wg_s[:, cols], wu_s[:, cols]], axis=1))
 
-    def near_copy(i, dst, rsem):
-        return pltpu.make_async_remote_copy(src_ref=nsend.at[i], dst_ref=dst.at[i], send_sem=ns_sem.at[i], recv_sem=rsem.at[i],
-                                            device_id=near_ok, device_id_type=MESH)
-
-    def far_copy(i):
-        return pltpu.make_async_remote_copy(src_ref=fsend.at[i], dst_ref=frecv.at[i], send_sem=fs_sem.at[i], recv_sem=fr_sem.at[i],
-                                            device_id=far_ok, device_id_type=MESH)
+    def sub(h):
+        return pl.ds(h * SUB, SUB)
+
+    def near_copy(i, h, dst, rsem):
+        return pltpu.make_async_remote_copy(src_ref=nsend.at[i, sub(h)], dst_ref=dst.at[i, sub(h)], send_sem=ns_sem.at[i, h],
+                                            recv_sem=rsem.at[i, h], device_id=near_ok, device_id_type=MESH)
+
+    def far_copy(i, h):
+        return pltpu.make_async_remote_copy(src_ref=fsend.at[i, sub(h)], dst_ref=frecv.at[i, sub(h)], send_sem=fs_sem.at[i, h],
+                                            recv_sem=fr_sem.at[i, h], device_id=far_ok, device_id_type=MESH)
 
     def m_copies(i):
         cb = (1 - nd) * NP + i
@@ -265,7 +271,8 @@
     def _():
         for i in range(NP):
             nsend[i] = piece(nd * NP + i)
-            near_copy(i, nrecv, nr_sem).start()
+            for h in range(NS):
+                near_copy(i, h, nrecv, nr_sem).start()
 
     for c in scp:
         c.wait_recv()
@@ -284,15 +291,19 @@
     def _():
         def near(i):
             mine = piece(nd * NP + i) * r_me2
-            near_copy(i, nrecv, nr_sem).wait_recv()
-            nsend[i] = nrecv[i] * r_end2 + mine
-            near_copy(i, frecv, fr_sem).start()
+            for h in range(NS):
+                near_copy(i, h, nrecv, nr_sem).wait_recv()
+                r = slice(h * SUB, (h + 1) * SUB)
+                nsend[i, r] = nrecv[i, r] * r_end2[r] + mine[r]
+                near_copy(i, h, frecv, fr_sem).start()
 
         def far(i):
             mine = piece((1 - nd) * NP + i) * r_me2
-            far_copy(i).wait_recv()
-            fsend[i] = frecv[i] + mine
-            far_copy(i).start()
+            for h in range(NS):
+                far_copy(i, h).wait_recv()
+                r = slice(h * SUB, (h + 1) * SUB)
+                fsend[i, r] = frecv[i, r] + mine[r]
+                far_copy(i, h).start()
 
         for i in range(NP + 2):
             if i < NP:
@@ -304,7 +315,8 @@
     def _():
         for i in range(NP):
             mine = piece((1 - nd) * NP + i) * r_me2
-            far_copy(i).wait_recv()
+            for h in range(NS):
+                far_copy(i, h).wait_recv()
             tot = frecv[i] + mine
             gate, up = tot[:, :PC], tot[:, PC:]
             m_all[(1 - nd) * NP + i] = (gate * (1.0 / (1.0 + jnp.exp(-gate))) * up).astype(BF16)
@@ -328,9 +340,7 @@
         d = dot(jnp.concatenate([m_all[2 * j], m_all[2 * j + 1]], axis=1), wd_s[2 * j * PC:2 * (j + 1) * PC, :])
         acc = d if acc is None else acc + d
     part2[...] = acc
-    tot = tp_scatter(part2, rs2_recv, rs2_send, rs2_rcv)
-    ho_all[my(t), :] = (h1_all[my(t), :].astype(F32) + tot.astype(BF16).astype(F32)).astype(BF16)
-    tp_gather(ho_all, ho_send, ho_recv)
+    tp_sum(part2, h1_all, dd2, ys2, yr2, ho_all, ar2)
     out[...] = ho_all[...]
     for c in pending:
         c.wait_send()
@@ -338,15 +348,17 @@
     @pl.when(end)
     def _():
         for i in range(NP):
-            near_copy(i, nrecv, nr_sem).wait_send()
+            for h in range(NS):
+                near_copy(i, h, nrecv, nr_sem).wait_send()
             for c in m_copies(i):
                 c.wait_send()
 
     @pl.when(mid)
     def _():
         for i in range(NP):
-            near_copy(i, frecv, fr_sem).wait_send()
-            far_copy(i).wait_send()
+            for h in range(NS):
+                near_copy(i, h, frecv, fr_sem).wait_send()
+                far_copy(i, h).wait_send()
 
 
 def local_layer(hidden, w_q, w_k, w_v, w_o, w_gate, w_up, w_down, norm_attn, norm_mlp, k_cache, v_cache, seq_lens, rope_cos, rope_sin):
@@ -374,36 +386,39 @@
     )(*hbm(hidden, norm_attn, w_q.transpose(1, 0, 2), w_k.reshape(2 * W, HD), w_v.reshape(2 * W, HD), rope_cos, rope_sin,
            k_cache.reshape(RB * SEQ2, HD), v_cache.reshape(RB * SEQ2, HD)))
 
-    o, k_out, v_out, _, _ = pl.pallas_call(
-        attn_kernel,
-        out_shape=(pltpu.VMEM((RB, W), BF16), jax.ShapeDtypeStruct((RB * SEQ2, HD), BF16), jax.ShapeDtypeStruct((RB * SEQ2, HD), BF16),
-                   pltpu.VMEM((RB * SEQ2, HD), BF16), pltpu.VMEM((RB * SEQ2, HD), BF16)),
-        in_specs=[SM, VM, VM, VM, VM, VM],
-        out_specs=(VM, ANY, ANY, VM, VM),
-        scratch_shapes=[pltpu.VMEM((RB, 8, HD), F32), DMA((2, RB))],
-        input_output_aliases={4: 3, 5: 4},
-        compiler_params=pltpu.CompilerParams(vmem_limit_bytes=40 * mib),
-        name='attn',
-    )(seq_lens, *vmem(q, kn, vn, kc, vc))
+    kc, vc = pl.pallas_call(
+        patch_kernel,
+        out_shape=(pltpu.VMEM((RB * SEQ2, HD), BF16), pltpu.VMEM((RB * SEQ2, HD), BF16)),
+        in_specs=[SM, VM, VM, VM, VM],
+        out_specs=(VM, VM),
+        input_output_aliases={3: 0, 4: 1},
+        compiler_params=pltpu.CompilerParams(vmem_limit_bytes=4 * mib),
+        name='patch',
+    )(seq_lens, *vmem(kn, vn, kc, vc))
 
     h_out = pl.pallas_call(
         tail_kernel,
         out_shape=jax.ShapeDtypeStruct((ROWS, W), BF16),
-        in_specs=[VM] + [ANY] * 6,
+        in_specs=[SM, VM, VM, VM] + [ANY] * 6,
         out_specs=VM,
         scratch_shapes=[
+            pltpu.VMEM((RB, 8, HD), F32), pltpu.VMEM((RB, W), BF16),
             pltpu.VMEM((NZ - 1, RB, W), BF16), pltpu.VMEM((ROWS, W), BF16), pltpu.VMEM((W,), BF16),
             pltpu.VMEM((W, W), BF16), pltpu.VMEM((W, FFL), BF16), pltpu.VMEM((W, FFL), BF16), pltpu.VMEM((FFL, W), BF16),
-            pltpu.VMEM((ROWS, W), F32), pltpu.VMEM((NT - 1, RB, W), F32), pltpu.VMEM((ROWS, W), BF16),
+            pltpu.VMEM((ROWS, W), F32), pltpu.VMEM((2, RB, W), F32), pltpu.VMEM((2, RB, W), F32), pltpu.VMEM((2, RB, W), F32),
+            pltpu.VMEM((ROWS, W), BF16),
             pltpu.VMEM((8, ROWS), F32), pltpu.VMEM((NZ - 1, 8, ROWS), F32),
             pltpu.VMEM((NP, ROWS, 2 * PC), F32), pltpu.VMEM((NP, ROWS, 2 * PC), F32), pltpu.VMEM((NP, ROWS, 2 * PC), F32),
             pltpu.VMEM((NP, ROWS, 2 * PC), F32), pltpu.VMEM((2 * NP, ROWS, PC), BF16),
-            pltpu.VMEM((ROWS, W), F32), pltpu.VMEM((NT - 1, RB, W), F32), pltpu.VMEM((ROWS, W), BF16),
-            DMA((6,)), DMA((3,)), DMA((3,)), DMA((3,)), DMA((3,)), DMA((3,)), DMA((3,)), DMA((3,)), DMA((3,)),
-            DMA((NP,)), DMA((NP,)), DMA((NP,)), DMA((NP,)), DMA((3, NP)), DMA((2 * NP,)), DMA((3,)), DMA((3,)), DMA((3,)), DMA((3,))],
+            pltpu.VMEM((ROWS, W), F32), pltpu.VMEM((2, RB, W), F32), pltpu.VMEM((2, RB, W), F32), pltpu.VMEM((2, RB, W), F32),
+            pltpu.VMEM((ROWS, W), BF16),
+            DMA((6,)), DMA((3, 2)), DMA((3, 2)), DMA((6, 2)), DMA((6, 2)), DMA((3,)), DMA((3,)),
+            DMA((NP, NS)), DMA((NP, NS)), DMA((NP, NS)), DMA((NP, NS)), DMA((3, NP)), DMA((2 * NP,))],
         compiler_params=pltpu.CompilerParams(collective_id=1, has_side_effects=True, vmem_limit_bytes=40 * mib),
+        cost_estimate=pl.CostEstimate(flops=40_000_000_000, bytes_accessed=30_000_000, transcendentals=0),
         name='tail',
-    )(*vmem(o), *hbm(hidden, norm_mlp, w_o.reshape(W, W), w_gate, w_up, w_down))
+    )(seq_lens, *vmem(q, kc, vc), *hbm(hidden, norm_mlp, w_o.reshape(W, W), w_gate, w_up, w_down))
+    k_out, v_out = kc, vc
     shape = (RB, SEQ2 // 2, 2, HD)
     return h_out, k_out.reshape(shape), v_out.reshape(shape)
 

time: 71.8 us -> 74.2 us (1.033)
  local copies, waits for them, and re-layouts: 0.64 us -> 7.45 us
  Pallas kernels: 70.3 us -> 65.9 us
    unnamed x1 -> x7, local copies, waits for them, and re-layouts: 0.64 us -> 7.45 us
    pallas_call x1, Pallas kernels: 7.19 us -> 0.66 us  [local_layer(): pl.pallas_call(patch_kernel, out_shape=(pltpu.VMEM((RB * SEQ2, HD), BF16)...]
    pallas_call x1, Pallas kernels: 48.2 us -> 50.4 us  [local_layer(): pl.pallas_call(tail_kernel, out_shape=jax.ShapeDtypeStruct((ROWS, W), BF1...]
where the time goes in v3:
time: 74.2 us; the launch traced here: 74 us
  Pallas kernels  65.9 us (89%)
  local copies, waits for them, and re-layouts  7.45 us (10%)
    pallas_call x1, Pallas kernels, local_layer(): pl.pallas_call(tail_kernel, out_shape=jax.ShapeDtypeStruct((ROWS, W), BF1...  50.4 us
    pallas_call x1, Pallas kernels, local_layer(): pl.pallas_call(qkv_kernel, out_shape=(pltpu.VMEM((RB, 8, HD), F32), pltpu...  14.9 us
    unnamed x7, local copies, waits for them, and re-layouts  7.45 us

profile of v3, /device:TPU:0, one launch (start us, length us, event | category | flops | bytes accessed | tf_op | source)
XLA Modules:
  0.0 74.0 jit_solution(8020280424397237658)
XLA Ops:
  0.6 0.0 copy-start
  0.6 14.9 %qkv.1 = (f32[16,8,128]{2,1,0:T(8,128)S(1)}, f32[16,8,128]{2,1,0:T(8,128)S(1)}, f32[16,8,128]{2,1,0:T(8,128)S(1)}, bf16[32768,128]{1,0:T(8,128)(2,1)S(1)}, bf16[32768,128]{1,0:T(8,128)(2,1)S(1)}) custom-call(bf16[64,768]{1,0:T(8,128)(2,1)} %hid.3, bf16[768]{0:T(1024)(128)(2,1)} %gain.2, bf16[6,768,128]{2,1,0:T(8,128)(2,1)} %bitcast.12, ...), custom_call_target="tpu_custom_call" | custom-call | tf_op jit(solution)/shard_map/qkv/pallas_call | solution.py:373
  15.5 0.0 copy-done
  15.5 0.7 patch.1
  16.2 50.4 %tail.1 = bf16[64,768]{1,0:T(8,128)(2,1)} custom-call(s32[16]{0:T(128)} %lens.3, f32[16,8,128]{2,1,0:T(8,128)S(1)} %get-tuple-element.10.q, bf16[32768,128]{1,0:T(8,128)(2,1)S(1)} %get-tuple-element.15.kc, bf16[32768,128]{1,0:T(8,128)(2,1)S(1)} %get-tuple-element.16.vc, bf16[64,768]{1,0:T(8,128)(2,1)} %hid.3, bf16[768]{0:T(1024)(128)(2,1)} %gain.3, ...), custom_call_target="tpu_custom_call" | custom-call | flops 40000000000 | bytes 30000000 | tf_op jit(solution)/shard_map/tail/pallas_call | solution.py:399
  66.6 3.4 %copy.26 = bf16[16,1024,2,128]{3,2,1,0:T(2,128)(2,1)} copy(bf16[16,1024,2,128]{3,2,1,0:T(2,128)(2,1)S(1)} %bitcast.9) | data formatting | bytes 16777216
  70.0 0.0 copy-start.1
  70.0 3.4 %copy.25 = bf16[16,1024,2,128]{3,2,1,0:T(2,128)(2,1)} copy(bf16[16,1024,2,128]{3,2,1,0:T(2,128)(2,1)S(1)} %bitcast.8) | data formatting | bytes 16777216
  73.4 0.0 copy-done.1
  73.4 0.6 copy.27
Async XLA Ops:
  0.6 14.9 %copy-start = (s32[16]{0:T(128)S(1)}, s32[16]{0:T(128)}, u32[]{:S(2)}) copy-start(s32[16]{0:T(128)} %lens.3) | copy-start | bytes 196
  70.0 3.4 %copy-start.1 = (bf16[64,768]{1,0:T(8,128)(2,1)S(1)}, bf16[64,768]{1,0:T(8,128)(2,1)}, u32[]{:S(2)}) copy-start(bf16[64,768]{1,0:T(8,128)(2,1)} %tail.1) | copy-start | bytes 294916

commit v4 on v3

--- a/solution.py
+++ b/solution.py
@@ -130,21 +130,50 @@
         c.wait()
 
 
-def patch_kernel(lens, kn, vn, kc, vc, kc_a, vc_a):
+def attn_kernel(lens, q, kn, vn, kc, vc, o, k_out, v_out, kc_a, vc_a, o_s, sem):
     del kc, vc
     r16 = lax.broadcasted_iota(jnp.int32, (16, HD), 0)
+    writes = []
     for b in range(RB):
         ln = lens[b]
         base = pl.multiple_of(b * SEQ2 + (ln // 8) * 16, 16)
         hit = (r16 // 2) == (ln % 8)
-        for new, cache in ((kn, kc_a), (vn, vc_a)):
+        for j, (new, cache, out) in enumerate(((kn, kc_a, k_out), (vn, vc_a, v_out))):
             fresh = jnp.concatenate([new[b], new[b]], axis=0)
             tile = cache[pl.ds(base, 16), :].astype(F32)
             cache[pl.ds(base, 16), :] = jnp.where(hit, fresh, tile).astype(BF16)
-
-
-def tail_kernel(lens, q, kc, vc, hid, gain, w_o, w_g, w_u, w_d, out,
-                o_s, o_mine, o_all, h_s, g_s, wo_s, wg_s, wu_s, wd_s, part, dd1, ys1, yr1, h1_all, st_send, st_recv,
+            rows = pl.ds(b * SEQ2, SEQ2)
+            w = pltpu.make_async_copy(cache.at[rows], out.at[rows], sem.at[j, b])
+            w.start()
+            writes.append(w)
+    row = lax.broadcasted_iota(jnp.int32, (16, SEQ2), 0)
+    col = lax.broadcasted_iota(jnp.int32, (16, SEQ2), 1)
+    same_head = (col % 2) == jnp.where(row % 8 < GRP, 0, 1)
+    slot = jnp.where(same_head, col // 2, SEQ2)
+    zero = jnp.zeros((8, HD), F32)
+    row1 = lax.broadcasted_iota(jnp.int32, (16, 1), 0)
+    for b in range(0, RB, 2):
+        lhs = jnp.concatenate([jnp.concatenate([q[b], zero], axis=1),
+                               jnp.concatenate([zero, q[b + 1]], axis=1)], axis=0).astype(BF16)
+        r0, r1 = pl.ds(b * SEQ2, SEQ2), pl.ds((b + 1) * SEQ2, SEQ2)
+        kk = jnp.concatenate([kc_a[r0, :], kc_a[r1, :]], axis=1)
+        s = lax.dot_general(lhs, kk, (((1,), (1,)), ((), ())), preferred_element_type=F32)
+        ln = jnp.where(row1 < 8, lens[b], lens[b + 1])
+        s = jnp.where(slot <= ln, s * (HD ** -0.5), -1e30)
+        e = jnp.exp(s - jnp.max(s, axis=1, keepdims=True))
+        pr = (e * (1.0 / jnp.sum(e, axis=1, keepdims=True))).astype(BF16)
+        vv = jnp.concatenate([vc_a[r0, :], vc_a[r1, :]], axis=1)
+        oo = dot(pr, vv)
+        o_s[b] = oo[:8, :HD]
+        o_s[b + 1] = oo[8:, HD:]
+    for hd in range(NH):
+        o[:, hd * HD:(hd + 1) * HD] = o_s[:, hd, :].astype(BF16)
+    for w in writes:
+        w.wait()
+
+
+def tail_kernel(o, hid, gain, w_o, w_g, w_u, w_d, out,
+                o_all, h_s, g_s, wo_s, wg_s, wu_s, wd_s, part, dd1, ys1, yr1, h1_all, st_send, st_recv,
                 nsend, fsend, nrecv, frecv, m_all, part2, dd2, ys2, yr2, ho_all,
                 w_sem, o_send, o_recv, ar1, ar2, st_ss, st_rs,
                 ns_sem, fs_sem, nr_sem, fr_sem, m_send, m_recv):
@@ -172,41 +201,13 @@
         return pl.ds(pl.multiple_of(i * RB, RB), RB)
 
     pending = []
-    row = lax.broadcasted_iota(jnp.int32, (16, SEQ2), 0)
-    column = lax.broadcasted_iota(jnp.int32, (16, SEQ2), 1)
-    same_head = (column % 2) == jnp.where(row % 8 < GRP, 0, 1)
-    slot = jnp.where(same_head, column // 2, SEQ2)
-    zero = jnp.zeros((8, HD), F32)
-    row1 = lax.broadcasted_iota(jnp.int32, (16, 1), 0)
-    cps = []
-    for half in range(2):
-        for b in range(8 * half, 8 * half + 8, 2):
-            lhs = jnp.concatenate([jnp.concatenate([q[b], zero], axis=1),
-                                   jnp.concatenate([zero, q[b + 1]], axis=1)], axis=0).astype(BF16)
-            r0, r1 = pl.ds(b * SEQ2, SEQ2), pl.ds((b + 1) * SEQ2, SEQ2)
-            kk = jnp.concatenate([kc[r0, :], kc[r1, :]], axis=1)
-            s = lax.dot_general(lhs, kk, (((1,), (1,)), ((), ())), preferred_element_type=F32)
-            ln = jnp.where(row1 < 8, lens[b], lens[b + 1])
-            s = jnp.where(slot <= ln, s * (HD ** -0.5), -1e30)
-            e = jnp.exp(s - jnp.max(s, axis=1, keepdims=True))
-            pr = (e * (1.0 / jnp.sum(e, axis=1, keepdims=True))).astype(BF16)
-            vv = jnp.concatenate([vc[r0, :], vc[r1, :]], axis=1)
-            oo = dot(pr, vv)
-            o_s[b] = oo[:8, :HD]
-            o_s[b + 1] = oo[8:, HD:]
-        rows = pl.ds(8 * half, 8)
-        for hd in range(NH):
-            o_mine[rows, hd * HD:(hd + 1) * HD] = o_s[rows, hd, :].astype(BF16)
-        if half == 0:
-            pl.semaphore_wait(barrier, 5)
-        cps.append([remote(o_mine.at[rows], o_all.at[k, rows], o_send.at[k, half], o_recv.at[k, half], {'dm': p})
-                    for k, p in enumerate(zp)])
+    pl.semaphore_wait(barrier, 5)
+    cps = [remote(o, o_all.at[k], o_send.at[k], o_recv.at[k], {'dm': p}) for k, p in enumerate(zp)]
+    pending += cps
     loads[0].wait()
-    part[my(z), :] = dot(o_mine[...], wo_s[...])
+    part[my(z), :] = dot(o[...], wo_s[...])
     for k in (2, 1, 0):
-        for half in range(2):
-            cps[half][k].wait_recv()
-            pending.append(cps[half][k])
+        cps[k].wait_recv()
         part[my(zp[k]), :] = dot(o_all[k], wo_s[...])
 
     def tp_sum(buf, base, dd, ys, yr, res, sems):
@@ -386,23 +387,24 @@
     )(*hbm(hidden, norm_attn, w_q.transpose(1, 0, 2), w_k.reshape(2 * W, HD), w_v.reshape(2 * W, HD), rope_cos, rope_sin,
            k_cache.reshape(RB * SEQ2, HD), v_cache.reshape(RB * SEQ2, HD)))
 
-    kc, vc = pl.pallas_call(
-        patch_kernel,
-        out_shape=(pltpu.VMEM((RB * SEQ2, HD), BF16), pltpu.VMEM((RB * SEQ2, HD), BF16)),
-        in_specs=[SM, VM, VM, VM, VM],
-        out_specs=(VM, VM),
-        input_output_aliases={3: 0, 4: 1},
-        compiler_params=pltpu.CompilerParams(vmem_limit_bytes=4 * mib),
-        name='patch',
-    )(seq_lens, *vmem(kn, vn, kc, vc))
+    o, k_out, v_out, _, _ = pl.pallas_call(
+        attn_kernel,
+        out_shape=(pltpu.VMEM((RB, W), BF16), jax.ShapeDtypeStruct((RB * SEQ2, HD), BF16), jax.ShapeDtypeStruct((RB * SEQ2, HD), BF16),
+                   pltpu.VMEM((RB * SEQ2, HD), BF16), pltpu.VMEM((RB * SEQ2, HD), BF16)),
+        in_specs=[SM, VM, VM, VM, VM, VM],
+        out_specs=(VM, ANY, ANY, VM, VM),
+        scratch_shapes=[pltpu.VMEM((RB, 8, HD), F32), DMA((2, RB))],
+        input_output_aliases={4: 3, 5: 4},
+        compiler_params=pltpu.CompilerParams(vmem_limit_bytes=40 * mib),
+        name='attn',
+    )(seq_lens, *vmem(q, kn, vn, kc, vc))
 
     h_out = pl.pallas_call(
         tail_kernel,
         out_shape=jax.ShapeDtypeStruct((ROWS, W), BF16),
-        in_specs=[SM, VM, VM, VM] + [ANY] * 6,
+        in_specs=[VM] + [ANY] * 6,
         out_specs=VM,
         scratch_shapes=[
-            pltpu.VMEM((RB, 8, HD), F32), pltpu.VMEM((RB, W), BF16),
             pltpu.VMEM((NZ - 1, RB, W), BF16), pltpu.VMEM((ROWS, W), BF16), pltpu.VMEM((W,), BF16),
             pltpu.VMEM((W, W), BF16), pltpu.VMEM((W, FFL), BF16), pltpu.VMEM((W, FFL), BF16), pltpu.VMEM((FFL, W), BF16),
             pltpu.VMEM((ROWS, W), F32), pltpu.VMEM((2, RB, W), F32), pltpu.VMEM((2, RB, W), F32), pltpu.VMEM((2, RB, W), F32),
@@ -412,13 +414,11 @@
             pltpu.VMEM((NP, ROWS, 2 * PC), F32), pltpu.VMEM((2 * NP, ROWS, PC), BF16),
             pltpu.VMEM((ROWS, W), F32), pltpu.VMEM((2, RB, W), F32), pltpu.VMEM((2, RB, W), F32), pltpu.VMEM((2, RB, W), F32),
             pltpu.VMEM((ROWS, W), BF16),
-            DMA((6,)), DMA((3, 2)), DMA((3, 2)), DMA((6, 2)), DMA((6, 2)), DMA((3,)), DMA((3,)),
+            DMA((6,)), DMA((3,)), DMA((3,)), DMA((6, 2)), DMA((6, 2)), DMA((3,)), DMA((3,)),
             DMA((NP, NS)), DMA((NP, NS)), DMA((NP, NS)), DMA((NP, NS)), DMA((3, NP)), DMA((2 * NP,))],
         compiler_params=pltpu.CompilerParams(collective_id=1, has_side_effects=True, vmem_limit_bytes=40 * mib),
-        cost_estimate=pl.CostEstimate(flops=40_000_000_000, bytes_accessed=30_000_000, transcendentals=0),
         name='tail',
-    )(seq_lens, *vmem(q, kc, vc), *hbm(hidden, norm_mlp, w_o.reshape(W, W), w_gate, w_up, w_down))
-    k_out, v_out = kc, vc
+    )(*vmem(o), *hbm(hidden, norm_mlp, w_o.reshape(W, W), w_gate, w_up, w_down))
     shape = (RB, SEQ2 // 2, 2, HD)
     return h_out, k_out.reshape(shape), v_out.reshape(shape)
 

time: 74.2 us -> 68.5 us (0.923)
  local copies, waits for them, and re-layouts: 7.45 us -> 0.64 us
  Pallas kernels: 65.9 us -> 67 us
    unnamed x7 -> x1, local copies, waits for them, and re-layouts: 7.45 us -> 0.64 us
    pallas_call x1, Pallas kernels: 0.66 us -> 7.19 us  [local_layer(): pl.pallas_call(attn_kernel, out_shape=(pltpu.VMEM((RB, W), BF16), jax.Sha...]
    pallas_call x1, Pallas kernels: 50.4 us -> 44.9 us  [local_layer(): pl.pallas_call(tail_kernel, out_shape=jax.ShapeDtypeStruct((ROWS, W), BF1...]
where the time goes in v4:
time: 68.5 us; the launch traced here: 68.3 us
  Pallas kernels  67 us (98%)
    pallas_call x1, Pallas kernels, local_layer(): pl.pallas_call(tail_kernel, out_shape=jax.ShapeDtypeStruct((ROWS, W), BF1...  44.9 us
    pallas_call x1, Pallas kernels, local_layer(): pl.pallas_call(qkv_kernel, out_shape=(pltpu.VMEM((RB, 8, HD), F32), pltpu...  14.9 us
    pallas_call x1, Pallas kernels, local_layer(): pl.pallas_call(attn_kernel, out_shape=(pltpu.VMEM((RB, W), BF16), jax.Sha...  7.19 us

profile of v4, /device:TPU:0, one launch (start us, length us, event | category | flops | bytes accessed | tf_op | source)
XLA Modules:
  0.0 68.3 jit_solution(3993754019095662966)
XLA Ops:
  0.6 14.9 %qkv.1 = (f32[16,8,128]{2,1,0:T(8,128)S(1)}, f32[16,8,128]{2,1,0:T(8,128)S(1)}, f32[16,8,128]{2,1,0:T(8,128)S(1)}, bf16[32768,128]{1,0:T(8,128)(2,1)S(1)}, bf16[32768,128]{1,0:T(8,128)(2,1)S(1)}) custom-call(bf16[64,768]{1,0:T(8,128)(2,1)} %hid.3, bf16[768]{0:T(1024)(128)(2,1)} %gain.2, bf16[6,768,128]{2,1,0:T(8,128)(2,1)} %bitcast.10, ...), custom_call_target="tpu_custom_call" | custom-call | tf_op jit(solution)/shard_map/qkv/pallas_call | solution.py:374
  15.5 7.2 %attn.1 = (bf16[16,768]{1,0:T(8,128)(2,1)S(1)}, bf16[32768,128]{1,0:T(8,128)(2,1)}, bf16[32768,128]{1,0:T(8,128)(2,1)}, bf16[32768,128]{1,0:T(8,128)(2,1)S(1)}, bf16[32768,128]{1,0:T(8,128)(2,1)S(1)}) custom-call(s32[16]{0:T(128)} %lens.1, f32[16,8,128]{2,1,0:T(8,128)S(1)} %get-tuple-element.11.q, ...), custom_call_target="tpu_custom_call", output_to_operand_aliasing={{3}: (4, {}), {4}: (5, {})} | custom-call | tf_op jit(solution)/shard_map/attn/pallas_call | solution.py:390
  22.7 44.9 %tail.1 = bf16[64,768]{1,0:T(8,128)(2,1)S(1)} custom-call(bf16[16,768]{1,0:T(8,128)(2,1)S(1)} %get-tuple-element.16.o, bf16[64,768]{1,0:T(8,128)(2,1)} %hid.3, bf16[768]{0:T(1024)(128)(2,1)} %gain.3, bf16[768,768]{1,0:T(8,128)(2,1)} %bitcast.11, bf16[768,2048]{1,0:T(8,128)(2,1)} %w_g.1, bf16[768,2048]{1,0:T(8,128)(2,1)} %w_u.1, bf16[2048,768]{1,0:T(8,128)(2,1)} %w_d.1), custom_call_target="tpu_custom_call" | custom-call | tf_op jit(solution)/shard_map/tail/pallas_call | solution.py:402
  67.7 0.6 copy.23
